TPU v7x, 32 devices: a whole 2x2x4 slice. The times are simulated.
32 devices in a mesh: tp: 4 (over z), cp: 2 (over y), dp: 4 (over x, core).
Axes of the slice: x: 2, y: 2, z: 4, core: 2. Of those that a mesh axis runs over, the one named last changes fastest.
Arguments:
- hidden: bfloat16 [128, 64, 2048], P('dp', 'cp')
- tokens: int32 [128, 64], P('dp', 'cp')
- seq_lens: int32 [128], P('dp')
- norm_gain: float32 [2048], replicated
- w_head: bfloat16 [2048, 49152], P(None, 'tp')
Outputs:
- output 1: float32 [128, 64], P('dp', 'cp')
- output 2: float32 [], replicated
- output 3: bfloat16 [128, 64, 2048], P('dp', 'cp')
- output 4: float32 [2048], replicated
- output 5: float32 [2048, 49152], P(None, 'tp')
All inputs are finite; a program needn't handle non-finite values.
Results may differ from a plain program's by a relative error of at most 0.001.
Values sent between devices are 32-bit elements.
A program may use at most 1 GiB of HBM per device.

v0:
```python
import jax
import jax.numpy as jnp
from jax import lax
from jax.sharding import PartitionSpec as P
from jax.experimental import pallas as pl
from jax.experimental.pallas import tpu as pltpu

NORM_EPS = 1e-5
F32, BF16 = jnp.float32, jnp.bfloat16
COLS = 512
TOK = 1024
VMEM = 63_000_000
MESH = pl.DeviceIdType.MESH


def _params(**kw):
    return pltpu.CompilerParams(vmem_limit_bytes=VMEM, **kw)


def _cost(flops, bytes_accessed):
    return pl.CostEstimate(flops=int(flops), bytes_accessed=int(bytes_accessed), transcendentals=0)


def _any():
    return pl.BlockSpec(memory_space=pl.ANY)


def _whole(shape):
    return pl.BlockSpec(shape, lambda *ids: (0,) * len(shape))


def _meet(peers):
    barrier = pltpu.get_barrier_semaphore()
    for peer in peers:
        pl.semaphore_signal(barrier, inc=1, device_id=peer, device_id_type=MESH)
    pl.semaphore_wait(barrier, len(peers))


def _send(src, dst, send_sem, recv_sem, peer):
    return pltpu.make_async_remote_copy(src, dst, send_sem, recv_sem, device_id=peer, device_id_type=MESH)


def _plane(n_dp):
    me = lax.axis_index('cp') * n_dp + lax.axis_index('dp')
    return me, lambda p: {'cp': p // n_dp, 'dp': p % n_dp}


def _columns(rows):
    return jnp.concatenate([rows, jnp.zeros((120, rows.shape[1]), F32)], axis=0).T


def _norm(hidden, gain):
    rows, width = hidden.shape
    step = 128
    n = rows // step

    def kernel(h_ref, g_ref, x_ref, xa_ref, xb_ref):
        i = pl.program_id(0)
        h = h_ref[...].astype(F32)
        inv_rms = lax.rsqrt(jnp.mean(h * h, axis=-1, keepdims=True) + NORM_EPS)
        x = (h * inv_rms * g_ref[...]).astype(BF16)
        x_ref[...] = x

        @pl.when(i < n // 2)
        def _():
            xa_ref[...] = x.astype(F32)

        @pl.when(i >= n // 2)
        def _():
            xb_ref[...] = x.astype(F32)

    half = jax.ShapeDtypeStruct((rows // 2, width), F32)
    return pl.pallas_call(
        kernel,
        grid=(n,),
        out_shape=[jax.ShapeDtypeStruct((rows, width), BF16), half, half],
        in_specs=[pl.BlockSpec((step, width), lambda i: (i, 0)), _whole((1, width))],
        out_specs=[
            pl.BlockSpec((step, width), lambda i: (i, 0)),
            pl.BlockSpec((step, width), lambda i: (jnp.minimum(i, n // 2 - 1), 0)),
            pl.BlockSpec((step, width), lambda i: (jnp.maximum(i - n // 2, 0), 0)),
        ],
        compiler_params=_params(),
        cost_estimate=_cost(rows * width * 256, rows * width * 8),
    )(hidden, gain)


def _logits(x, row, count, w, n_tp, n_dp):
    rows, width = x.shape
    vocab = w.shape[1]
    cols = 1024
    steps = vocab // cols

    def kernel(x_ref, row_ref, cnt_ref, cnt_any, w_ref, z_ref, mrow_ref, mcol_ref, m_ref, s_ref, t_ref, lab_ref, st_buf, cnt_buf, cs_sem, cr_sem, ss_sem, sr_sem):
        i = pl.program_id(0)
        tp, dp = lax.axis_index('tp'), lax.axis_index('dp')

        def tell(k):
            return _send(cnt_any, cnt_buf.at[k - 1], cs_sem.at[k - 1], cr_sem.at[k - 1], {'dp': (dp + k) % n_dp})

        def give(k, slot):
            return _send(st_buf.at[slot], st_buf.at[slot], ss_sem.at[k - 1], sr_sem.at[k - 1], {'tp': (tp + k) % n_tp})

        @pl.when(i == 0)
        def _():
            _meet([{'tp': (tp + k) % n_tp} for k in range(1, n_tp)] + [{'dp': (dp + k) % n_dp} for k in range(1, n_dp)])
            for k in range(1, n_dp):
                tell(k).start()
            m_ref[...] = jnp.full_like(m_ref, -jnp.inf)
            s_ref[...] = jnp.zeros_like(s_ref)
            t_ref[...] = jnp.zeros_like(t_ref)
            lab_ref[...] = _columns(row_ref[...])

        z = jnp.dot(x_ref[...], w_ref[...], preferred_element_type=F32)
        z_ref[...] = z
        rel = lab_ref[:, 0:1].astype(jnp.int32) - (tp * vocab + cols * i)
        lane = lax.broadcasted_iota(jnp.int32, (rows, 128), 1)
        old = m_ref[...]
        top = old
        for g in range(cols // 128):
            top = jnp.maximum(top, z[:, g * 128:(g + 1) * 128])
        total = s_ref[...] * jnp.exp(old - top)
        target = t_ref[...]
        for g in range(cols // 128):
            z_g = z[:, g * 128:(g + 1) * 128]
            total = total + jnp.exp(z_g - top)
            target = target + jnp.where(lane == rel - g * 128, z_g, 0.0)
        m_ref[...] = top
        s_ref[...] = total
        t_ref[...] = target

        @pl.when(i == steps - 1)
        def _():
            top, total = m_ref[...], s_ref[...]
            row_max = jnp.max(top, axis=1, keepdims=True)
            row_sum = jnp.sum(total * jnp.exp(top - row_max), axis=1, keepdims=True)
            row_target = jnp.sum(t_ref[...], axis=1, keepdims=True)
            st_buf[tp] = jnp.where(lane == 0, row_max, jnp.where(lane == 1, row_sum, row_target)).T[0:8]
            for k in range(1, n_dp):
                tell(k).wait()
            for k in range(1, n_tp):
                give(k, tp).start()
            n_valid = cnt_ref[0:1, 0:1]
            for k in range(1, n_dp):
                n_valid = n_valid + cnt_buf[k - 1, 0:1, 0:1]
            for k in range(1, n_tp):
                give(k, tp).wait_send()
                give(k, (tp + n_tp - k) % n_tp).wait_recv()
            top = st_buf[0, 0:1]
            for k in range(1, n_tp):
                top = jnp.maximum(top, st_buf[k, 0:1])
            total = st_buf[0, 1:2] * jnp.exp(st_buf[0, 0:1] - top)
            target = st_buf[0, 2:3]
            for k in range(1, n_tp):
                total = total + st_buf[k, 1:2] * jnp.exp(st_buf[k, 0:1] - top)
                target = target + st_buf[k, 2:3]
            lse = top + jnp.log(total)
            valid = row_ref[1:2]
            sub = lax.broadcasted_iota(jnp.int32, (8, rows), 0)
            meta = jnp.where(sub == 0, lse, jnp.where(sub == 1, row_ref[0:1], jnp.where(sub == 2, valid / n_valid, jnp.where(sub == 3, (lse - target) * valid, n_valid))))
            mrow_ref[...] = meta
            mcol_ref[...] = _columns(meta)

    return pl.pallas_call(
        kernel,
        grid=(steps,),
        out_shape=[jax.ShapeDtypeStruct((rows, vocab), F32), jax.ShapeDtypeStruct((8, rows), F32), jax.ShapeDtypeStruct((rows, 128), F32)],
        in_specs=[_whole((rows, width)), _whole((8, rows)), _whole((8, 128)), _any(), pl.BlockSpec((width, cols), lambda i: (0, i))],
        out_specs=[pl.BlockSpec((rows, cols), lambda i: (0, i)), _whole((8, rows)), _whole((rows, 128))],
        scratch_shapes=[pltpu.VMEM((rows, 128), F32)] * 4
        + [pltpu.VMEM((n_tp, 8, rows), F32), pltpu.VMEM((n_dp - 1, 8, 128), F32)]
        + [pltpu.SemaphoreType.DMA((n_dp - 1,))] * 2 + [pltpu.SemaphoreType.DMA((n_tp - 1,))] * 2,
        compiler_params=_params(collective_id=1, has_side_effects=True),
        cost_estimate=_cost(2 * rows * width * vocab, vocab * (2 * width + 4 * rows)),
    )(x, row, count, count, w)


def _d_logits(z, meta, first):
    rel = meta[:, 1:2].astype(jnp.int32) - first
    hit = lax.broadcasted_iota(jnp.int32, z.shape, 1) == rel
    return ((jnp.exp(z - meta[:, 0:1]) - jnp.where(hit, 1.0, 0.0)) * meta[:, 2:3]).astype(BF16)


def _d_norm(z, mcol, mrow, w, n_cp, n_dp):
    rows, vocab = z.shape
    width = w.shape[0]
    cols = 1024
    steps = vocab // cols
    groups = n_cp * n_dp

    def kernel(z_ref, mcol_ref, mrow_any, w_ref, acc_ref, all_ref, buf, own_sem, send_sem, recv_sem):
        i = pl.program_id(0)
        me, device = _plane(n_dp)
        own = pltpu.make_async_copy(mrow_any, buf.at[me], own_sem)

        def give(e, slot):
            return _send(mrow_any, buf.at[slot], send_sem.at[e - 1], recv_sem.at[e - 1], device((me + e) % groups))

        @pl.when(i == 0)
        def _():
            own.start()
            _meet([device((me + e) % groups) for e in range(1, groups)])
            for e in range(1, groups):
                give(e, me).start()
            acc_ref[...] = jnp.zeros_like(acc_ref)

        d = _d_logits(z_ref[...], mcol_ref[...], lax.axis_index('tp') * vocab + i * cols)
        acc_ref[...] += lax.dot_general(d, w_ref[...], (((1,), (1,)), ((), ())), preferred_element_type=F32)

        @pl.when(i == steps - 1)
        def _():
            own.wait()
            for e in range(1, groups):
                give(e, me).wait_send()
                give(e, (me + groups - e) % groups).wait_recv()
            all_ref[...] = buf[...]

    return pl.pallas_call(
        kernel,
        grid=(steps,),
        out_shape=[jax.ShapeDtypeStruct((rows, width), F32), jax.ShapeDtypeStruct((groups, 8, rows), F32)],
        in_specs=[pl.BlockSpec((rows, cols), lambda i: (0, i)), _whole((rows, 128)), _any(), pl.BlockSpec((width, cols), lambda i: (0, i))],
        out_specs=[_whole((rows, width)), _whole((groups, 8, rows))],
        scratch_shapes=[pltpu.VMEM((groups, 8, rows), F32), pltpu.SemaphoreType.DMA] + [pltpu.SemaphoreType.DMA((groups - 1,))] * 2,
        compiler_params=_params(collective_id=2, has_side_effects=True),
        cost_estimate=_cost(2 * rows * width * vocab, vocab * (2 * width + 4 * rows)),
    )(z, mcol, mrow, w)


class _Split:
    def __init__(self, vocab, groups):
        self.vocab, self.groups = vocab, groups
        self.blocks = vocab // COLS
        self.n_f = (self.blocks - groups - 2) // 2
        self.g0 = 2 * self.n_f
        self.r0 = self.g0 + groups
        self.n = 1 + self.n_f

    def block(self, b, me, core):
        return jnp.where(b == 0, self.g0 + me, core * self.n_f + b - 1)


def _part(x_b, meta, w, first):
    rows = jnp.concatenate([meta[k] for k in range(meta.shape[0])], axis=1) if meta.shape[0] > 1 else meta[0]
    d = _d_logits(jnp.dot(x_b, w, preferred_element_type=F32), _columns(rows), first)
    return lax.dot_general(x_b, d, (((0,), (0,)), ((), ())), preferred_element_type=F32)


def _head_a(x, meta, w, d_x_norm, split, n_tp, n_dp):
    rows, width = x.shape
    half = meta.shape[2] // 2
    n_tok = rows // TOK
    sub = d_x_norm.shape[0] // n_tp

    def kernel(x_ref, meta_ref, w_ref, dx_any, acc_ref, xb_ref, got_any, leg, mid, send_sem, recv_sem, leg_sem, mid_sem):
        b, i = pl.program_id(0), pl.program_id(1)
        tp = lax.axis_index('tp')
        me, _ = _plane(n_dp)
        inner = (tp == 1) | (tp == 2)
        far = jnp.where(tp < 2, 3, 0)

        def quarter(q):
            return dx_any.at[pl.ds(pl.multiple_of(q * sub, 8), sub)]

        def give(to, src):
            return _send(src, got_any.at[tp], send_sem.at[to], recv_sem.at[tp], {'tp': to})

        def arrive(frm):
            return _send(mid, got_any.at[frm], send_sem.at[frm], recv_sem.at[frm], {'tp': frm})

        first_leg = _send(quarter(far), leg, leg_sem.at[0], leg_sem.at[1], {'tp': jnp.where(tp == 0, 1, 2)})
        load_mid = pltpu.make_async_copy(quarter(far), mid, mid_sem)

        @pl.when((b == 0) & (i == 0))
        def _():
            _meet([{'tp': (tp + k) % n_tp} for k in range(1, n_tp)])

            @pl.when(inner)
            def _():
                load_mid.start()
                give(3 - tp, quarter(3 - tp)).start()
                give(3 - far, quarter(3 - far)).start()

            @pl.when(jnp.logical_not(inner))
            def _():
                first_leg.start()
                for gap in (2, 1):
                    to = jnp.where(tp == 0, gap, 3 - gap)
                    give(to, quarter(to)).start()

        @pl.when((b == split.n // 2 - 1) & (i == 0) & inner)
        def _():
            load_mid.wait()
            first_leg.wait_recv()
            mid[...] += leg[...]

        @pl.when((b == split.n // 2 - 1) & (i == 1) & inner)
        def _():
            give(far, mid).start()

        @pl.when(i == 0)
        def _():
            acc_ref[...] = jnp.zeros_like(acc_ref)

        x_b = x_ref[...].astype(BF16)

        @pl.when(b == 0)
        def _():
            xb_ref[...] = x_b

        first = tp * split.vocab + split.block(b, me, lax.axis_index('dp') % 2) * COLS
        acc_ref[...] += _part(x_b, meta_ref, w_ref[...], first)

        @pl.when((b == split.n - 1) & (i == n_tok - 1))
        def _():
            @pl.when(inner)
            def _():
                for q in range(n_tp):
                    @pl.when(tp != q)
                    def _():
                        give(q, mid).wait_send()
                        arrive(q).wait_recv()

            @pl.when(jnp.logical_not(inner))
            def _():
                first_leg.wait_send()
                for q in (1, 2):
                    give(q, mid).wait_send()
                    arrive(q).wait_recv()

    return pl.pallas_call(
        kernel,
        grid=(split.n, n_tok),
        out_shape=[jax.ShapeDtypeStruct((width, split.n * COLS), F32), jax.ShapeDtypeStruct((2 * rows, width), BF16), jax.ShapeDtypeStruct((n_tp, sub, width), F32)],
        in_specs=[
            pl.BlockSpec((TOK, width), lambda b, i: (i, 0)),
            pl.BlockSpec((TOK // half, 8, half), lambda b, i: (i, 0, 0)),
            pl.BlockSpec((width, COLS), lambda b, i: (0, split.block(b, _plane(n_dp)[0], lax.axis_index('dp') % 2))),
            _any(),
        ],
        out_specs=[pl.BlockSpec((width, COLS), lambda b, i: (0, b)), pl.BlockSpec((TOK, width), lambda b, i: (jnp.where(b == 0, i, n_tok - 1), 0)), _any()],
        scratch_shapes=[pltpu.VMEM((sub, width), F32)] * 2 + [pltpu.SemaphoreType.DMA((n_tp,))] * 2 + [pltpu.SemaphoreType.DMA((2,)), pltpu.SemaphoreType.DMA],
        compiler_params=_params(collective_id=3, has_side_effects=True),
        cost_estimate=_cost(4 * rows * width * split.n * COLS, split.n * rows * width * 4),
    )(x, meta, w, d_x_norm)


def _head_g(x, meta, w, part, x_all, split, n_dp):
    rows, width = x.shape
    half = meta.shape[2] // 2
    n_tok = rows // half

    def kernel(x_ref, meta_ref, w_ref, init_ref, _, acc_ref, xb_ref):
        @pl.when(pl.program_id(0) == 0)
        def _():
            acc_ref[...] = init_ref[...]

        x_b = x_ref[...].astype(BF16)
        xb_ref[...] = x_b
        first = lax.axis_index('tp') * split.vocab + (split.g0 + _plane(n_dp)[0]) * COLS
        acc_ref[...] += _part(x_b, meta_ref, w_ref[...], first)

    return pl.pallas_call(
        kernel,
        grid=(n_tok,),
        out_shape=[jax.ShapeDtypeStruct((width, COLS), F32), jax.ShapeDtypeStruct((2 * rows, width), BF16)],
        in_specs=[
            pl.BlockSpec((half, width), lambda i: (i, 0)),
            pl.BlockSpec((1, 8, half), lambda i: (i, 0, 1)),
            pl.BlockSpec((width, COLS), lambda i: (0, split.g0 + _plane(n_dp)[0])),
            _whole((width, COLS)),
            _any(),
        ],
        out_specs=[_whole((width, COLS)), pl.BlockSpec((half, width), lambda i: (n_tok + i, 0))],
        input_output_aliases={4: 1},
        compiler_params=_params(),
        cost_estimate=_cost(4 * rows * width * COLS, rows * width * 6),
    )(x, meta, w, part, x_all)


def _head_f(x, meta, w, part, d_hid, d_gain, split, n_tp, n_cp, n_dp):
    width = x.shape[1]
    rows = x.shape[0] // 2
    half = meta.shape[2] // 2
    n_f, groups = split.n_f, n_cp * n_dp
    n_tok = rows // TOK
    sub = d_hid.shape[0]

    def kernel(x_ref, meta_ref, w_ref, init_any, dh_any, dg_any, out_any, dhall_any, dg_ref, acc, dg_z, dg_s, dg_x, init_sem, own_sem, send_sem, recv_sem, hs_sem, hr_sem, fs_sem, zs_sem, zr_sem, zo_sem, xs_sem, xr_sem):
        j, i = pl.program_id(0), pl.program_id(1)
        tp, dp = lax.axis_index('tp'), lax.axis_index('dp')
        me, device = _plane(n_dp)
        core = dp % 2
        slot = j % 2
        z_peers = [{'tp': (tp + k) % n_tp} for k in range(1, n_tp)]

        def at(owner, jj):
            return out_any.at[:, pl.ds(pl.multiple_of((owner * n_f + jj) * COLS, COLS), COLS)]

        def init(jj):
            return pltpu.make_async_copy(init_any.at[:, pl.ds(pl.multiple_of((jj + 1) * COLS, COLS), COLS)], acc.at[jj % 2], init_sem.at[jj % 2])

        def own(jj):
            return pltpu.make_async_copy(acc.at[jj % 2], at(core, jj), own_sem.at[jj % 2])

        def swap(jj, owner):
            return _send(acc.at[jj % 2], at(owner, jj), send_sem.at[jj % 2], recv_sem.at[jj], {'dp': dp + 1 - 2 * core})

        def hid(to):
            return _send(dh_any, dhall_any.at[tp], hs_sem.at[to], hr_sem.at[tp], {'tp': to})

        def relay(row, to):
            return _send(dhall_any.at[row], dhall_any.at[row], fs_sem, hr_sem.at[row], {'tp': to})

        def gain_z(k, row):
            return _send(dg_any, dg_z.at[row], zs_sem.at[k - 1], zr_sem.at[k - 1], z_peers[k - 1])

        def gain_x(e, row):
            return _send(dg_s, dg_x.at[row], xs_sem.at[e - 1], xr_sem.at[e - 1], device((me + e) % groups))

        gain_own = pltpu.make_async_copy(dg_any, dg_z.at[tp], zo_sem)

        def each_near(act):
            for gap in (2, 1):
                for to in (tp + gap, tp - gap):
                    @pl.when((to >= 0) & (to < n_tp))
                    def _():
                        getattr(hid(to), act)()

        @pl.when((j == 0) & (i == 0))
        def _():
            init(0).start()
            gain_own.start()
            _meet(z_peers + [device((me + e) % groups) for e in range(1, groups)])
            for k in range(1, n_tp):
                gain_z(k, tp).start()
            each_near('start')

        @pl.when((j == 1) & (i == 0))
        def _():
            gain_own.wait()
            for k in range(1, n_tp):
                gain_z(k, tp).wait_send()
                gain_z(k, (tp + n_tp - k) % n_tp).wait_recv()
            total = dg_z[0]
            for k in range(1, n_tp):
                total = total + dg_z[k]
            dg_s[...] = total
            dg_x[me] = total

        @pl.when((j == 1) & (i == n_tok - 1))
        def _():
            for e in range(1, groups):
                gain_x(e, me).start()

        @pl.when((j == n_f // 2 + 1) & (i == 0))
        def _():
            @pl.when(tp == 2)
            def _():
                relay(0, 3).wait_recv()
                relay(0, 3).start()

            @pl.when(tp == 1)
            def _():
                relay(3, 0).wait_recv()
                relay(3, 0).start()

        @pl.when(i == 0)
        def _():
            init(j).wait()

        @pl.when(i == n_tok // 2)
        def _():
            @pl.when(j >= 1)
            def _():
                own(j - 1).wait()
                swap(j - 1, core).wait_send()

            @pl.when(j < n_f - 1)
            def _():
                init(j + 1).start()

        first = tp * split.vocab + (core * n_f + j) * COLS
        acc[slot] += _part(x_ref[...], meta_ref, w_ref[...], first)

        @pl.when(i == n_tok - 1)
        def _():
            own(j).start()
            swap(j, core).start()

        @pl.when((j == n_f - 1) & (i == n_tok - 1))
        def _():
            for e in range(1, groups):
                gain_x(e, me).wait_send()
                gain_x(e, (me + groups - e) % groups).wait_recv()
            total = dg_x[0]
            for e in range(1, groups):
                total = total + dg_x[e]
            dg_ref[...] = total
            own(j).wait()
            swap(j, core).wait_send()
            for jj in range(n_f):
                swap(jj, 1 - core).wait_recv()
            each_near('wait_send')

            @pl.when((tp == 1) | (tp == 2))
            def _():
                relay(0, 0).wait_send()

            for row in range(n_tp):
                relayed = ((tp == 2) & (row == 0)) | ((tp == 1) & (row == 3))

                @pl.when((row != tp) & jnp.logical_not(relayed))
                def _():
                    relay(row, tp).wait_recv()

    return pl.pallas_call(
        kernel,
        grid=(n_f, n_tok),
        out_shape=[jax.ShapeDtypeStruct((width, 2 * n_f * COLS), F32), jax.ShapeDtypeStruct((n_tp, sub, width), F32), jax.ShapeDtypeStruct((8, width), F32)],
        in_specs=[
            pl.BlockSpec((TOK, width), lambda j, i: (n_tok + i, 0)),
            pl.BlockSpec((TOK // half, 8, half), lambda j, i: (i, 0, 1)),
            pl.BlockSpec((width, COLS), lambda j, i: (0, lax.axis_index('dp') % 2 * n_f + j)),
            _any(),
            _any(),
            _any(),
        ],
        out_specs=[_any(), _any(), _whole((8, width))],
        scratch_shapes=[pltpu.VMEM((2, width, COLS), F32), pltpu.VMEM((n_tp, 8, width), F32), pltpu.VMEM((8, width), F32), pltpu.VMEM((groups, 8, width), F32)]
        + [pltpu.SemaphoreType.DMA((2,))] * 3 + [pltpu.SemaphoreType.DMA((n_f,)), pltpu.SemaphoreType.DMA((n_tp,)), pltpu.SemaphoreType.DMA((n_tp,)), pltpu.SemaphoreType.DMA]
        + [pltpu.SemaphoreType.DMA((n_tp - 1,))] * 2 + [pltpu.SemaphoreType.DMA] + [pltpu.SemaphoreType.DMA((groups - 1,))] * 2,
        compiler_params=_params(collective_id=4, has_side_effects=True),
        cost_estimate=_cost(4 * rows * width * n_f * COLS, n_f * rows * width * 2),
    )(x, meta, w, part, d_hid, d_gain)


def _head_r(x, meta, w, head_f, head_g, split):
    rows, width = x.shape
    half = meta.shape[2] // 2
    vocab, groups = split.vocab, split.groups
    steps = 2 * groups
    f_wide, r_wide = split.g0 * COLS, 2 * COLS
    strip = width // steps

    def kernel(x_ref, meta_ref, w_ref, f_any, g_any, out_any, acc, f_buf, g_buf, own_sem, in_sem, out_sem):
        i = pl.program_id(0)
        own = pltpu.make_async_copy(acc, out_any.at[:, pl.ds(split.r0 * COLS, r_wide)], own_sem)

        def places(s):
            at = pl.ds(pl.multiple_of(s * strip, 8), strip)
            g_from = pl.ds(pl.multiple_of(s * (width // 2), 8), width // 2)
            g_rows = pl.ds(pl.multiple_of(s % 2 * (width // 2), 8), width // 2)
            g_cols = pl.ds(pl.multiple_of((split.g0 + s // 2) * COLS, COLS), COLS)
            return f_any.at[at], out_any.at[at, pl.ds(0, f_wide)], g_any.at[g_from], out_any.at[g_rows, g_cols]

        def load(s):
            f_src, _, g_src, _ = places(s)
            return (pltpu.make_async_copy(f_src, f_buf.at[s % 2], in_sem.at[0, s % 2]),
                    pltpu.make_async_copy(g_src, g_buf.at[s % 2], in_sem.at[1, s % 2]))

        def store(s):
            _, f_dst, _, g_dst = places(s)
            return (pltpu.make_async_copy(f_buf.at[s % 2], f_dst, out_sem.at[0, s % 2]),
                    pltpu.make_async_copy(g_buf.at[s % 2], g_dst, out_sem.at[1, s % 2]))

        def each(copies, act):
            for c in copies:
                getattr(c, act)()

        @pl.when(i == 0)
        def _():
            each(load(0), 'start')
            acc[...] = jnp.zeros_like(acc)

        @pl.when(i >= 1)
        def _():
            each(load(i - 1), 'wait')
            each(store(i - 1), 'start')

            @pl.when(i >= 2)
            def _():
                each(store(i - 2), 'wait')

            each(load(i), 'start')

        acc[...] += _part(x_ref[...], meta_ref, w_ref[...], lax.axis_index('tp') * vocab + split.r0 * COLS)

        @pl.when(i == steps - 1)
        def _():
            own.start()
            each(load(i), 'wait')
            each(store(i), 'start')
            each(store(i - 1), 'wait')
            each(store(i), 'wait')
            own.wait()

    return pl.pallas_call(
        kernel,
        grid=(steps,),
        out_shape=jax.ShapeDtypeStruct((width, vocab), F32),
        in_specs=[
            pl.BlockSpec((half, width), lambda i: (i, 0)),
            pl.BlockSpec((1, 8, half), lambda i: (i % groups, 0, i // groups)),
            pl.BlockSpec((width, r_wide), lambda i: (0, split.r0 // 2)),
            _any(),
            _any(),
        ],
        out_specs=_any(),
        scratch_shapes=[pltpu.VMEM((width, r_wide), F32), pltpu.VMEM((2, strip, f_wide), F32), pltpu.VMEM((2, width // 2, COLS), F32)]
        + [pltpu.SemaphoreType.DMA] + [pltpu.SemaphoreType.DMA((2, 2))] * 2,
        compiler_params=_params(),
        cost_estimate=_cost(4 * rows * width * r_wide, width * vocab * 8),
    )(x, meta, w, head_f, head_g)


def _finish(hidden, d_x_norm, got, gain, n_tp):
    rows, width = hidden.shape
    sub = rows // n_tp
    step = 64
    n = sub // step

    def kernel(h_ref, own_ref, got_ref, g_ref, dh_ref, dg_ref):
        @pl.when(pl.program_id(0) == 0)
        def _():
            dg_ref[...] = jnp.zeros_like(dg_ref)

        h = h_ref[...].astype(F32)
        inv_rms = lax.rsqrt(jnp.mean(h * h, axis=-1, keepdims=True) + NORM_EPS)
        x = h * inv_rms
        d = own_ref[...]
        tp = lax.axis_index('tp')
        for q in range(n_tp):
            d = d + jnp.where((q != tp) & (q - tp < 3) & (tp - q < 3), got_ref[q], 0.0)
        dg_ref[0:1] += jnp.sum(d * x, axis=0, keepdims=True)
        d_x = d * g_ref[...]
        dh_ref[...] = (inv_rms * (d_x - x * jnp.mean(d_x * x, axis=-1, keepdims=True))).astype(BF16).astype(F32)

    return pl.pallas_call(
        kernel,
        grid=(n,),
        out_shape=[jax.ShapeDtypeStruct((sub, width), F32), jax.ShapeDtypeStruct((8, width), F32)],
        in_specs=[
            pl.BlockSpec((step, width), lambda i: (lax.axis_index('tp') * n + i, 0)),
            pl.BlockSpec((step, width), lambda i: (lax.axis_index('tp') * n + i, 0)),
            pl.BlockSpec((n_tp, step, width), lambda i: (0, i, 0)),
            _whole((1, width)),
        ],
        out_specs=[pl.BlockSpec((step, width), lambda i: (i, 0)), _whole((8, width))],
        compiler_params=_params(),
        cost_estimate=_cost(sub * width * 256, sub * width * 24),
    )(hidden, d_x_norm, got, gain)


def _join(own, got, n_tp):
    sub, width = own.shape

    def kernel(own_ref, got_ref, o_ref):
        o_ref[...] = jnp.where(pl.program_id(0) == lax.axis_index('tp'), own_ref[...], got_ref[0]).astype(BF16)

    return pl.pallas_call(
        kernel,
        grid=(n_tp,),
        out_shape=jax.ShapeDtypeStruct((n_tp * sub, width), BF16),
        in_specs=[_whole((sub, width)), pl.BlockSpec((1, sub, width), lambda q: (q, 0, 0))],
        out_specs=pl.BlockSpec((sub, width), lambda q: (q, 0)),
        compiler_params=_params(),
        cost_estimate=_cost(n_tp * sub * width * 256, n_tp * sub * width * 6),
    )(own, got)


def solution(mesh):
    n_tp, n_cp, n_dp = mesh.shape['tp'], mesh.shape['cp'], mesh.shape['dp']
    groups = n_cp * n_dp

    def part_fn(hidden, tokens, seq_lens, norm_gain, w_head):
        n_seq, local_len, width = hidden.shape
        n_tok = n_seq * local_len
        seg_len = local_len // 2
        split = _Split(w_head.shape[1], groups)
        cp_rank = lax.axis_index('cp')
        gain = norm_gain.reshape(1, width)
        hidden_rows = hidden.reshape(n_tok, width)

        x_norm, send_a, send_b = _norm(hidden_rows, gain)
        x_a = lax.all_gather(send_a, ('cp', 'dp'), axis=0, tiled=True)
        x_b = lax.all_gather(send_b, ('cp', 'dp'), axis=0, tiled=True)

        edge = lax.ppermute(jnp.where(cp_rank == 0, tokens[:, seg_len], tokens[:, 0]), 'cp', [(0, 1), (1, 0)])
        first_end = jnp.where(cp_rank == 0, edge, tokens[:, seg_len])
        second_end = jnp.where(cp_rank == 0, 0, edge)
        labels = jnp.concatenate([tokens[:, 1:seg_len], first_end[:, None], tokens[:, seg_len + 1:], second_end[:, None]], axis=1)
        seg_pos = jnp.arange(seg_len)
        positions = jnp.concatenate([cp_rank * seg_len + seg_pos, (2 * n_cp - 1 - cp_rank) * seg_len + seg_pos])
        valid = (positions[None, :] + 1 < seq_lens[:, None]).astype(F32)
        row = jnp.concatenate([labels.astype(F32).reshape(1, n_tok), valid.reshape(1, n_tok), jnp.zeros((6, n_tok), F32)])
        count = jnp.broadcast_to(jnp.sum(seq_lens - 1).astype(F32), (8, 128))

        logits, meta_row, meta_col = _logits(x_norm, row, count, w_head, n_tp, n_dp)
        d_x_norm, meta = _d_norm(logits, meta_col, meta_row, w_head, n_cp, n_dp)
        tok_loss = meta_row[3].reshape(n_seq, local_len)
        loss_mean = jnp.sum(meta[:, 3]) / meta[0, 4, 0]
        meta, tok_loss, loss_mean = lax.optimization_barrier((meta, tok_loss, loss_mean))
        part, x_all, got = _head_a(x_a, meta, w_head, d_x_norm, split, n_tp, n_dp)
        d_hid, d_gain = _finish(hidden_rows, d_x_norm, got, gain, n_tp)
        d_head_g, x_all = _head_g(x_b, meta, w_head, part, x_all, split, n_dp)
        d_head_g = lax.all_gather(d_head_g, ('cp', 'dp'), axis=0, tiled=True)
        d_head_f, d_hid_all, d_gain = _head_f(x_all, meta, w_head, part, d_hid, d_gain, split, n_tp, n_cp, n_dp)
        d_hidden = _join(d_hid, d_hid_all, n_tp)
        d_head = _head_r(x_all, meta, w_head, d_head_f, d_head_g, split)
        return tok_loss, loss_mean, d_hidden.reshape(hidden.shape), d_gain[0], d_head

    return jax.shard_map(part_fn, mesh=mesh, in_specs=(P('dp', 'cp', None), P('dp', 'cp'), P('dp'), P(None), P(None, 'tp')), out_specs=(P('dp', 'cp'), P(), P('dp', 'cp', None), P(None), P(None, 'tp')), check_vma=False)
```

profile of v0, /device:TPU:11, one launch (start us, length us, event | category | flops | bytes accessed | tf_op | source)
XLA Modules:
  0.0 702.3 jit_solution(18334284609814979179)
XLA Ops:
  7.2 9.1 %shard_map.92 = (bf16[1024,2048]{1,0:T(8,128)(2,1)}, f32[512,2048]{1,0:T(8,128)}, f32[512,2048]{1,0:T(8,128)}) custom-call(bf16[1024,2048]{1,0:T(8,128)(2,1)} %bitcast.9, f32[1,2048]{1,0:T(1,128)} %bitcast.12), custom_call_target="tpu_custom_call" | custom-call | flops 536870912 | bytes 16777216 | tf_op jit(solution)/shard_map/pallas_call | solution.py:73
  16.3 0.0 all-gather.6.cloned.1.call-start
  16.4 0.7 all-gather.6.cloned.1.call-update
  17.1 0.0 all-gather.8.cloned.1.call-start
  17.1 1.0 slice_reduce_fusion.1
  18.1 1.3 collective-permute-start
  19.4 1.3 add_reduce_fusion
  21.4 0.1 add_add_fusion
  21.5 0.7 compare_convert_fusion
  22.2 0.1 reshape.77
  22.3 0.9 fusion.2
  23.1 0.1 pad.2.clone
  23.2 0.1 copy.13
  23.3 0.1 copy.14
  23.4 0.1 add_convert_fusion
  23.5 0.1 convert_element_type.30
  23.6 0.7 maximum_maximum_fusion.row_ref
  24.3 0.6 broadcast_in_dim.22.cnt_ref.cnt_any
  24.9 75.9 %shard_map.93 = (f32[1024,12288]{1,0:T(8,128)}, f32[8,1024]{1,0:T(8,128)}, f32[1024,128]{1,0:T(8,128)}) custom-call(bf16[1024,2048]{1,0:T(8,128)(2,1)} %get-tuple-element.26.x_ref, f32[8,1024]{1,0:T(8,128)} %maximum_maximum_fusion.row_ref, f32[8,128]{1,0:T(8,128)} %broadcast_in_dim.22.cnt_ref.cnt_any, f32[8,128]{1,0:T(8,128)} %broadcast_in_dim.22.cnt_ref.cnt_any, ...), custom_call_target="tpu_custom_call" | custom-call | flops 51539607552 | bytes 100663296 | tf_op jit(solution)/shard_map/pallas_call | solution.py:164
  100.7 72.1 %shard_map.94 = (f32[1024,2048]{1,0:T(8,128)}, f32[8,8,1024]{2,1,0:T(8,128)}) custom-call(f32[1024,12288]{1,0:T(8,128)} %get-tuple-element.27.z_ref, f32[1024,128]{1,0:T(8,128)} %get-tuple-element.28.mcol_ref, f32[8,1024]{1,0:T(8,128)} %get-tuple-element.29.mrow_any, bf16[2048,12288]{1,0:T(8,128)(2,1)} %w_ref.11), custom_call_target="tpu_custom_call" | custom-call | flops 51539607552 | bytes 100663296 | tf_op jit(solution)/shard_map/pallas_call | solution.py:218
  172.8 1.2 slice.31
  174.0 0.8 slice_reduce_fusion.3
  174.8 0.7 reshape_squeeze.3
  175.5 1.6 slice_reduce_fusion
  178.4 3.1 all-gather.4.cloned.1.call-done.x_ref
  181.5 196.9 %shard_map.95 = (f32[2048,4096]{1,0:T(8,128)}, bf16[8192,2048]{1,0:T(8,128)(2,1)}, f32[4,256,2048]{2,1,0:T(8,128)}) custom-call(f32[4096,2048]{1,0:T(8,128)} %all-gather.4.cloned.1.call-done.x_ref, f32[8,8,1024]{2,1,0:T(8,128)} %get-tuple-element.35.meta_ref, bf16[2048,12288]{1,0:T(8,128)(2,1)} %w_ref.11, f32[1024,2048]{1,0:T(8,128)} %get-tuple-element.33.dx_any.own_ref), custom_call_target="tpu_custom_call" | custom-call | flops 137438953472 | bytes 268435456 | tf_op jit(solution)/shard_map/pallas_call | solution.py:331
  378.4 27.4 %shard_map.97 = (f32[2048,512]{1,0:T(8,128)}, bf16[8192,2048]{1,0:T(8,128)(2,1)}) custom-call(f32[4096,2048]{1,0:T(8,128)} %all-gather.6.cloned.1.call-done.x_ref, f32[8,8,1024]{2,1,0:T(8,128)} %get-tuple-element.35.meta_ref, bf16[2048,12288]{1,0:T(8,128)(2,1)} %w_ref.11, ...), custom_call_target="tpu_custom_call", output_to_operand_aliasing={{1}: (4, {})} | custom-call | flops 17179869184 | bytes 50331648 | tf_op jit(solution)/shard_map/pallas_call | solution.py:363
  405.8 6.9 shard_map.96
  412.7 185.3 %shard_map.98 = (f32[2048,7168]{1,0:T(8,128)}, f32[4,256,2048]{2,1,0:T(8,128)}, f32[8,2048]{1,0:T(8,128)}) custom-call(bf16[8192,2048]{1,0:T(8,128)(2,1)} %get-tuple-element.41.x_ref, f32[8,8,1024]{2,1,0:T(8,128)} %get-tuple-element.35.meta_ref, bf16[2048,12288]{1,0:T(8,128)(2,1)} %w_ref.11, f32[2048,4096]{1,0:T(8,128)} %get-tuple-element.39.init_ref.init_any, ...), custom_call_target="tpu_custom_call" | custom-call | flops 120259084288 | bytes 117440512 | tf_op jit(solution)/shard_map/pallas_call | solution.py:517
  598.0 1.4 slice.32
  599.5 6.6 shard_map.99
  606.0 88.6 %shard_map.100 = f32[2048,12288]{1,0:T(8,128)} custom-call(bf16[8192,2048]{1,0:T(8,128)(2,1)} %get-tuple-element.41.x_ref, f32[8,8,1024]{2,1,0:T(8,128)} %get-tuple-element.35.meta_ref, bf16[2048,12288]{1,0:T(8,128)(2,1)} %w_ref.11, f32[2048,7168]{1,0:T(8,128)} %get-tuple-element.45.f_any, f32[16384,512]{1,0:T(8,128)} %all-gather.8.cloned.1.call-done.g_any), custom_call_target="tpu_custom_call" | custom-call | flops 68719476736 | bytes 201326592 | tf_op jit(solution)/shard_map/pallas_call | solution.py:598
  (11 shorter events, 0.1 us)
Async XLA Ops:
  7.2 174.3 %all-gather.4.cloned.1.call-start = ((), (), s32[]{:S(2)}) async-start(), calls=%async_computation | async-start | bytes 37748736 | tf_op jit(solution)/shard_map/all_gather | solution.py:686
  16.3 362.1 %all-gather.6.cloned.1.call-start = ((), (), s32[]{:S(2)}) async-start(), calls=%async_computation.1 | async-start | bytes 37748736 | tf_op jit(solution)/shard_map/all_gather | solution.py:687
  17.1 589.0 %all-gather.8.cloned.1.call-start = ((), (), s32[]{:S(2)}) async-start(), calls=%async_computation.2 | async-start | bytes 37748736 | tf_op jit(solution)/shard_map/all_gather | solution.py:707
  18.1 5.1 collective-permute-start
Sparse Core Ops, SparseCore 0:
  16.4 165.0 all-gather.3
  183.4 160.6 all-gather.5
  406.0 170.6 all-gather.7
where the time goes:
time: 703 us; the launch traced here: 702 us
  Pallas kernels  669 us (95%)
  between operations  17 us (2%)
    pallas_call x1, Pallas kernels, _head_a(): pl.pallas_call(kernel, grid=(split.n, n_tok), out_shape=[jax.ShapeDtypeSt...  197 us
    pallas_call x1, Pallas kernels, _head_f(): pl.pallas_call(kernel, grid=(n_f, n_tok), out_shape=[jax.ShapeDtypeStruct...  185 us
    pallas_call x1, Pallas kernels, _head_r(): pl.pallas_call(kernel, grid=(steps,), out_shape=jax.ShapeDtypeStruct((wid...  88.6 us
    pallas_call x1, Pallas kernels, _logits(): pl.pallas_call(kernel, grid=(steps,), out_shape=[jax.ShapeDtypeStruct((ro...  75.9 us
    pallas_call x1, Pallas kernels, _d_norm(): pl.pallas_call(kernel, grid=(steps,), out_shape=[jax.ShapeDtypeStruct((ro...  72.1 us
    pallas_call x1, Pallas kernels, _head_g(): pl.pallas_call(kernel, grid=(n_tok,), out_shape=[jax.ShapeDtypeStruct((wi...  27.4 us
  transfers between devices with their start and end apart: 4, of which 1 were waited for; matrix products, arithmetic and copies ran while one was open for 2% of the time, Pallas kernels for 77%

commit v1 on v0

--- a/solution.py
+++ b/solution.py
@@ -49,40 +49,30 @@
     return jnp.concatenate([rows, jnp.zeros((120, rows.shape[1]), F32)], axis=0).T
 
 
-def _norm(hidden, gain):
+def _norm(hidden, gain, half, x_norm=None):
     rows, width = hidden.shape
     step = 128
-    n = rows // step
-
-    def kernel(h_ref, g_ref, x_ref, xa_ref, xb_ref):
-        i = pl.program_id(0)
+    n = rows // 2 // step
+
+    def kernel(h_ref, g_ref, *refs):
+        x_ref, xs_ref = refs[-2:]
         h = h_ref[...].astype(F32)
         inv_rms = lax.rsqrt(jnp.mean(h * h, axis=-1, keepdims=True) + NORM_EPS)
         x = (h * inv_rms * g_ref[...]).astype(BF16)
         x_ref[...] = x
-
-        @pl.when(i < n // 2)
-        def _():
-            xa_ref[...] = x.astype(F32)
-
-        @pl.when(i >= n // 2)
-        def _():
-            xb_ref[...] = x.astype(F32)
-
-    half = jax.ShapeDtypeStruct((rows // 2, width), F32)
+        xs_ref[...] = x.astype(F32)
+
+    at = pl.BlockSpec((step, width), lambda i: (half * n + i, 0))
     return pl.pallas_call(
         kernel,
         grid=(n,),
-        out_shape=[jax.ShapeDtypeStruct((rows, width), BF16), half, half],
-        in_specs=[pl.BlockSpec((step, width), lambda i: (i, 0)), _whole((1, width))],
-        out_specs=[
-            pl.BlockSpec((step, width), lambda i: (i, 0)),
-            pl.BlockSpec((step, width), lambda i: (jnp.minimum(i, n // 2 - 1), 0)),
-            pl.BlockSpec((step, width), lambda i: (jnp.maximum(i - n // 2, 0), 0)),
-        ],
+        out_shape=[jax.ShapeDtypeStruct((rows, width), BF16), jax.ShapeDtypeStruct((rows // 2, width), F32)],
+        in_specs=[at, _whole((1, width))] + [_any()] * (x_norm is not None),
+        out_specs=[at, pl.BlockSpec((step, width), lambda i: (i, 0))],
+        input_output_aliases={2: 0} if x_norm is not None else {},
         compiler_params=_params(),
-        cost_estimate=_cost(rows * width * 256, rows * width * 8),
-    )(hidden, gain)
+        cost_estimate=_cost(rows * width * 128, rows * width * 4),
+    )(*((hidden, gain) if x_norm is None else (hidden, gain, x_norm)))
 
 
 def _logits(x, row, count, w, n_tp, n_dp):
@@ -254,6 +244,8 @@
 
     def kernel(x_ref, meta_ref, w_ref, dx_any, acc_ref, xb_ref, got_any, leg, mid, send_sem, recv_sem, leg_sem, mid_sem):
         b, i = pl.program_id(0), pl.program_id(1)
+        step = b * n_tok + i
+        stage = [split.n * n_tok * part // 32 for part in (10, 12)]
         tp = lax.axis_index('tp')
         me, _ = _plane(n_dp)
         inner = (tp == 1) | (tp == 2)
@@ -284,17 +276,20 @@
             @pl.when(jnp.logical_not(inner))
             def _():
                 first_leg.start()
-                for gap in (2, 1):
-                    to = jnp.where(tp == 0, gap, 3 - gap)
-                    give(to, quarter(to)).start()
-
-        @pl.when((b == split.n // 2 - 1) & (i == 0) & inner)
+
+        @pl.when((step == stage[0]) & jnp.logical_not(inner))
+        def _():
+            for gap in (1, 2):
+                to = jnp.where(tp == 0, gap, 3 - gap)
+                give(to, quarter(to)).start()
+
+        @pl.when((step == stage[1]) & inner)
         def _():
             load_mid.wait()
             first_leg.wait_recv()
             mid[...] += leg[...]
 
-        @pl.when((b == split.n // 2 - 1) & (i == 1) & inner)
+        @pl.when((step == stage[1] + 1) & inner)
         def _():
             give(far, mid).start()
 
@@ -388,7 +383,10 @@
 
     def kernel(x_ref, meta_ref, w_ref, init_any, dh_any, dg_any, out_any, dhall_any, dg_ref, acc, dg_z, dg_s, dg_x, init_sem, own_sem, send_sem, recv_sem, hs_sem, hr_sem, fs_sem, zs_sem, zr_sem, zo_sem, xs_sem, xr_sem):
         j, i = pl.program_id(0), pl.program_id(1)
+        step = j * n_tok + i
+        stage = [n_f * n_tok * part // 28 for part in (9, 12, 18, 21)]
         tp, dp = lax.axis_index('tp'), lax.axis_index('dp')
+        inner = (tp == 1) | (tp == 2)
         me, device = _plane(n_dp)
         core = dp % 2
         slot = j % 2
@@ -406,11 +404,13 @@
         def swap(jj, owner):
             return _send(acc.at[jj % 2], at(owner, jj), send_sem.at[jj % 2], recv_sem.at[jj], {'dp': dp + 1 - 2 * core})
 
-        def hid(to):
-            return _send(dh_any, dhall_any.at[tp], hs_sem.at[to], hr_sem.at[tp], {'tp': to})
-
-        def relay(row, to):
-            return _send(dhall_any.at[row], dhall_any.at[row], fs_sem, hr_sem.at[row], {'tp': to})
+        def hid(to, h):
+            rows_h = pl.ds(h * (sub // 2), sub // 2)
+            return _send(dh_any.at[rows_h], dhall_any.at[tp, rows_h], hs_sem.at[to, h], hr_sem.at[tp, h], {'tp': to})
+
+        def relay(row, to, h):
+            at_h = dhall_any.at[row, pl.ds(h * (sub // 2), sub // 2)]
+            return _send(at_h, at_h, fs_sem.at[h], hr_sem.at[row, h], {'tp': to})
 
         def gain_z(k, row):
             return _send(dg_any, dg_z.at[row], zs_sem.at[k - 1], zr_sem.at[k - 1], z_peers[k - 1])
@@ -420,12 +420,16 @@
 
         gain_own = pltpu.make_async_copy(dg_any, dg_z.at[tp], zo_sem)
 
-        def each_near(act):
-            for gap in (2, 1):
-                for to in (tp + gap, tp - gap):
-                    @pl.when((to >= 0) & (to < n_tp))
-                    def _():
-                        getattr(hid(to), act)()
+        def across(h, act):
+            getattr(hid(jnp.where(tp < 2, tp + 2, tp - 2), h), act)()
+
+        def beside(inward, act):
+            for h in range(2):
+                getattr(hid(jnp.where((tp < 2) == inward, tp + 1, tp - 1), h), act)()
+
+        def pass_on(h):
+            relay(3 * (2 - tp), 3 * (tp - 1), h).wait_recv()
+            relay(3 * (2 - tp), 3 * (tp - 1), h).start()
 
         @pl.when((j == 0) & (i == 0))
         def _():
@@ -434,7 +438,27 @@
             _meet(z_peers + [device((me + e) % groups) for e in range(1, groups)])
             for k in range(1, n_tp):
                 gain_z(k, tp).start()
-            each_near('start')
+            across(0, 'start')
+
+            @pl.when(inner)
+            def _():
+                beside(False, 'start')
+
+        @pl.when(step == stage[0])
+        def _():
+            across(1, 'start')
+
+        @pl.when((step == stage[1]) & inner)
+        def _():
+            pass_on(0)
+
+        @pl.when(step == stage[2])
+        def _():
+            beside(True, 'start')
+
+        @pl.when((step == stage[3]) & inner)
+        def _():
+            pass_on(1)
 
         @pl.when((j == 1) & (i == 0))
         def _():
@@ -452,18 +476,6 @@
         def _():
             for e in range(1, groups):
                 gain_x(e, me).start()
-
-        @pl.when((j == n_f // 2 + 1) & (i == 0))
-        def _():
-            @pl.when(tp == 2)
-            def _():
-                relay(0, 3).wait_recv()
-                relay(0, 3).start()
-
-            @pl.when(tp == 1)
-            def _():
-                relay(3, 0).wait_recv()
-                relay(3, 0).start()
 
         @pl.when(i == 0)
         def _():
@@ -501,18 +513,23 @@
             swap(j, core).wait_send()
             for jj in range(n_f):
                 swap(jj, 1 - core).wait_recv()
-            each_near('wait_send')
-
-            @pl.when((tp == 1) | (tp == 2))
-            def _():
-                relay(0, 0).wait_send()
+            for h in range(2):
+                across(h, 'wait_send')
+            beside(True, 'wait_send')
+
+            @pl.when(inner)
+            def _():
+                beside(False, 'wait_send')
+                for h in range(2):
+                    relay(0, 0, h).wait_send()
 
             for row in range(n_tp):
                 relayed = ((tp == 2) & (row == 0)) | ((tp == 1) & (row == 3))
 
                 @pl.when((row != tp) & jnp.logical_not(relayed))
                 def _():
-                    relay(row, tp).wait_recv()
+                    for h in range(2):
+                        relay(row, tp, h).wait_recv()
 
     return pl.pallas_call(
         kernel,
@@ -528,22 +545,25 @@
         ],
         out_specs=[_any(), _any(), _whole((8, width))],
         scratch_shapes=[pltpu.VMEM((2, width, COLS), F32), pltpu.VMEM((n_tp, 8, width), F32), pltpu.VMEM((8, width), F32), pltpu.VMEM((groups, 8, width), F32)]
-        + [pltpu.SemaphoreType.DMA((2,))] * 3 + [pltpu.SemaphoreType.DMA((n_f,)), pltpu.SemaphoreType.DMA((n_tp,)), pltpu.SemaphoreType.DMA((n_tp,)), pltpu.SemaphoreType.DMA]
+        + [pltpu.SemaphoreType.DMA((2,))] * 3 + [pltpu.SemaphoreType.DMA((n_f,)), pltpu.SemaphoreType.DMA((n_tp, 2)), pltpu.SemaphoreType.DMA((n_tp, 2)), pltpu.SemaphoreType.DMA((2,))]
         + [pltpu.SemaphoreType.DMA((n_tp - 1,))] * 2 + [pltpu.SemaphoreType.DMA] + [pltpu.SemaphoreType.DMA((groups - 1,))] * 2,
         compiler_params=_params(collective_id=4, has_side_effects=True),
         cost_estimate=_cost(4 * rows * width * n_f * COLS, n_f * rows * width * 2),
     )(x, meta, w, part, d_hid, d_gain)
 
 
-def _head_r(x, meta, w, head_f, head_g, split):
+def _head_r(x, meta, w, head_f, head_g, d_hid, d_hid_all, split, n_tp):
     rows, width = x.shape
     half = meta.shape[2] // 2
     vocab, groups = split.vocab, split.groups
     steps = 2 * groups
     f_wide, r_wide = split.g0 * COLS, 2 * COLS
     strip = width // steps
-
-    def kernel(x_ref, meta_ref, w_ref, f_any, g_any, out_any, acc, f_buf, g_buf, own_sem, in_sem, out_sem):
+    per_q = steps // n_tp
+    sub = d_hid.shape[0]
+    piece = sub // per_q
+
+    def kernel(x_ref, meta_ref, w_ref, f_any, g_any, dh_ref, dhall_ref, out_any, hid_ref, acc, f_buf, g_buf, own_sem, in_sem, out_sem):
         i = pl.program_id(0)
         own = pltpu.make_async_copy(acc, out_any.at[:, pl.ds(split.r0 * COLS, r_wide)], own_sem)
 
@@ -584,6 +604,7 @@
 
             each(load(i), 'start')
 
+        hid_ref[...] = jnp.where(i // per_q == lax.axis_index('tp'), dh_ref[...], dhall_ref[0]).astype(BF16)
         acc[...] += _part(x_ref[...], meta_ref, w_ref[...], lax.axis_index('tp') * vocab + split.r0 * COLS)
 
         @pl.when(i == steps - 1)
@@ -598,20 +619,22 @@
     return pl.pallas_call(
         kernel,
         grid=(steps,),
-        out_shape=jax.ShapeDtypeStruct((width, vocab), F32),
+        out_shape=[jax.ShapeDtypeStruct((width, vocab), F32), jax.ShapeDtypeStruct((n_tp * sub, width), BF16)],
         in_specs=[
             pl.BlockSpec((half, width), lambda i: (i, 0)),
             pl.BlockSpec((1, 8, half), lambda i: (i % groups, 0, i // groups)),
             pl.BlockSpec((width, r_wide), lambda i: (0, split.r0 // 2)),
             _any(),
             _any(),
+            pl.BlockSpec((piece, width), lambda i: (i % per_q, 0)),
+            pl.BlockSpec((1, piece, width), lambda i: (i // per_q, i % per_q, 0)),
         ],
-        out_specs=_any(),
+        out_specs=[_any(), pl.BlockSpec((piece, width), lambda i: (i, 0))],
         scratch_shapes=[pltpu.VMEM((width, r_wide), F32), pltpu.VMEM((2, strip, f_wide), F32), pltpu.VMEM((2, width // 2, COLS), F32)]
         + [pltpu.SemaphoreType.DMA] + [pltpu.SemaphoreType.DMA((2, 2))] * 2,
         compiler_params=_params(),
         cost_estimate=_cost(4 * rows * width * r_wide, width * vocab * 8),
-    )(x, meta, w, head_f, head_g)
+    )(x, meta, w, head_f, head_g, d_hid, d_hid_all)
 
 
 def _finish(hidden, d_x_norm, got, gain, n_tp):
@@ -652,23 +675,6 @@
     )(hidden, d_x_norm, got, gain)
 
 
-def _join(own, got, n_tp):
-    sub, width = own.shape
-
-    def kernel(own_ref, got_ref, o_ref):
-        o_ref[...] = jnp.where(pl.program_id(0) == lax.axis_index('tp'), own_ref[...], got_ref[0]).astype(BF16)
-
-    return pl.pallas_call(
-        kernel,
-        grid=(n_tp,),
-        out_shape=jax.ShapeDtypeStruct((n_tp * sub, width), BF16),
-        in_specs=[_whole((sub, width)), pl.BlockSpec((1, sub, width), lambda q: (q, 0, 0))],
-        out_specs=pl.BlockSpec((sub, width), lambda q: (q, 0)),
-        compiler_params=_params(),
-        cost_estimate=_cost(n_tp * sub * width * 256, n_tp * sub * width * 6),
-    )(own, got)
-
-
 def solution(mesh):
     n_tp, n_cp, n_dp = mesh.shape['tp'], mesh.shape['cp'], mesh.shape['dp']
     groups = n_cp * n_dp
@@ -682,8 +688,9 @@
         gain = norm_gain.reshape(1, width)
         hidden_rows = hidden.reshape(n_tok, width)
 
-        x_norm, send_a, send_b = _norm(hidden_rows, gain)
+        x_norm, send_a = _norm(hidden_rows, gain, 0)
         x_a = lax.all_gather(send_a, ('cp', 'dp'), axis=0, tiled=True)
+        x_norm, send_b = _norm(hidden_rows, gain, 1, x_norm)
         x_b = lax.all_gather(send_b, ('cp', 'dp'), axis=0, tiled=True)
 
         edge = lax.ppermute(jnp.where(cp_rank == 0, tokens[:, seg_len], tokens[:, 0]), 'cp', [(0, 1), (1, 0)])
@@ -702,12 +709,13 @@
         loss_mean = jnp.sum(meta[:, 3]) / meta[0, 4, 0]
         meta, tok_loss, loss_mean = lax.optimization_barrier((meta, tok_loss, loss_mean))
         part, x_all, got = _head_a(x_a, meta, w_head, d_x_norm, split, n_tp, n_dp)
+        d_head_g, x_all = _head_g(x_b, meta, w_head, part, x_all, split, n_dp)
+        got, d_head_g = lax.optimization_barrier((got, d_head_g))
+        d_head_g = lax.all_gather(d_head_g, ('cp', 'dp'), axis=0, tiled=True)
         d_hid, d_gain = _finish(hidden_rows, d_x_norm, got, gain, n_tp)
-        d_head_g, x_all = _head_g(x_b, meta, w_head, part, x_all, split, n_dp)
-        d_head_g = lax.all_gather(d_head_g, ('cp', 'dp'), axis=0, tiled=True)
         d_head_f, d_hid_all, d_gain = _head_f(x_all, meta, w_head, part, d_hid, d_gain, split, n_tp, n_cp, n_dp)
-        d_hidden = _join(d_hid, d_hid_all, n_tp)
-        d_head = _head_r(x_all, meta, w_head, d_head_f, d_head_g, split)
+        d_head, d_hidden = _head_r(x_all, meta, w_head, d_head_f, d_head_g, d_hid, d_hid_all, split, n_tp)
+
         return tok_loss, loss_mean, d_hidden.reshape(hidden.shape), d_gain[0], d_head
 
     return jax.shard_map(part_fn, mesh=mesh, in_specs=(P('dp', 'cp', None), P('dp', 'cp'), P('dp'), P(None), P(None, 'tp')), out_specs=(P('dp', 'cp'), P(), P('dp', 'cp', None), P(None), P(None, 'tp')), check_vma=False)

time: 703 us -> 677 us (0.963)
  the two profiles are of different devices: /device:TPU:11 before, /device:TPU:1 now
where the time goes in v1:
time: 677 us; the launch traced here: 676 us
  Pallas kernels  648 us (96%)
  between operations  17 us (3%)
    pallas_call x1, Pallas kernels, _head_a(): pl.pallas_call(kernel, grid=(split.n, n_tok), out_shape=[jax.ShapeDtypeSt...  198 us
    pallas_call x1, Pallas kernels, _head_f(): pl.pallas_call(kernel, grid=(n_f, n_tok), out_shape=[jax.ShapeDtypeStruct...  163 us
    pallas_call x1, Pallas kernels, _head_r(): pl.pallas_call(kernel, grid=(steps,), out_shape=[jax.ShapeDtypeStruct((wi...  93.1 us
    pallas_call x1, Pallas kernels, _logits(): pl.pallas_call(kernel, grid=(steps,), out_shape=[jax.ShapeDtypeStruct((ro...  77.3 us
    pallas_call x1, Pallas kernels, _d_norm(): pl.pallas_call(kernel, grid=(steps,), out_shape=[jax.ShapeDtypeStruct((ro...  72.3 us
    pallas_call x1, Pallas kernels, _head_g(): pl.pallas_call(kernel, grid=(n_tok,), out_shape=[jax.ShapeDtypeStruct((wi...  27.4 us
  transfers between devices with their start and end apart: 4, of which 0 were waited for; matrix products, arithmetic and copies ran while one was open for 1% of the time, Pallas kernels for 77%

profile of v1, /device:TPU:1, one launch (start us, length us, event | category | flops | bytes accessed | tf_op | source)
XLA Modules:
  0.0 675.9 jit_solution(17746427820961387437)
XLA Ops:
  7.2 0.0 all-gather.6.cloned.1.call-start
  7.2 5.1 shard_map.92
  12.3 0.0 all-gather.4.cloned.1.call-start
  12.4 5.1 shard_map.93
  17.5 0.0 all-gather.8.cloned.1.call-start
  17.6 0.2 slice_reduce_fusion.1
  17.8 2.1 collective-permute-start
  19.9 0.6 add_reduce_fusion
  21.2 0.1 add_add_fusion
  21.3 0.1 compare_convert_fusion
  21.4 0.1 reshape.77
  21.5 0.1 fusion.2
  21.5 0.1 pad.2.clone
  21.6 0.1 copy.14
  21.7 0.1 copy.15
  21.8 0.1 add_convert_fusion
  21.9 0.1 convert_element_type.30
  22.0 0.7 maximum_maximum_fusion.row_ref
  22.7 0.6 broadcast_in_dim.22.cnt_ref.cnt_any
  23.2 77.3 %shard_map.94 = (f32[1024,12288]{1,0:T(8,128)}, f32[8,1024]{1,0:T(8,128)}, f32[1024,128]{1,0:T(8,128)}) custom-call(bf16[1024,2048]{1,0:T(8,128)(2,1)} %get-tuple-element.32.x_ref, f32[8,1024]{1,0:T(8,128)} %maximum_maximum_fusion.row_ref, f32[8,128]{1,0:T(8,128)} %broadcast_in_dim.22.cnt_ref.cnt_any, f32[8,128]{1,0:T(8,128)} %broadcast_in_dim.22.cnt_ref.cnt_any, ...), custom_call_target="tpu_custom_call" | custom-call | flops 51539607552 | bytes 100663296 | tf_op jit(solution)/shard_map/pallas_call | solution.py:154
  100.5 72.3 %shard_map.95 = (f32[1024,2048]{1,0:T(8,128)}, f32[8,8,1024]{2,1,0:T(8,128)}) custom-call(f32[1024,12288]{1,0:T(8,128)} %get-tuple-element.33.z_ref, f32[1024,128]{1,0:T(8,128)} %get-tuple-element.34.mcol_ref, f32[8,1024]{1,0:T(8,128)} %get-tuple-element.35.mrow_any, bf16[2048,12288]{1,0:T(8,128)(2,1)} %w_ref.11), custom_call_target="tpu_custom_call" | custom-call | flops 51539607552 | bytes 100663296 | tf_op jit(solution)/shard_map/pallas_call | solution.py:208
  172.8 1.2 slice.31
  174.0 0.8 slice_reduce_fusion.3
  174.8 0.7 reshape_squeeze.3
  175.5 1.6 slice_reduce_fusion
  178.5 0.0 all-gather.6.cloned.1.call-done.x_ref
  178.5 197.9 %shard_map.96 = (f32[2048,4096]{1,0:T(8,128)}, bf16[8192,2048]{1,0:T(8,128)(2,1)}, f32[4,256,2048]{2,1,0:T(8,128)}) custom-call(f32[4096,2048]{1,0:T(8,128)} %all-gather.6.cloned.1.call-done.x_ref, f32[8,8,1024]{2,1,0:T(8,128)} %get-tuple-element.40.meta_ref, bf16[2048,12288]{1,0:T(8,128)(2,1)} %w_ref.11, f32[1024,2048]{1,0:T(8,128)} %get-tuple-element.42.dx_any.own_ref), custom_call_target="tpu_custom_call" | custom-call | flops 137438953472 | bytes 268435456 | tf_op jit(solution)/shard_map/pallas_call | solution.py:326
  376.5 27.4 %shard_map.97 = (f32[2048,512]{1,0:T(8,128)}, bf16[8192,2048]{1,0:T(8,128)(2,1)}) custom-call(f32[4096,2048]{1,0:T(8,128)} %all-gather.4.cloned.1.call-done.x_ref, f32[8,8,1024]{2,1,0:T(8,128)} %get-tuple-element.40.meta_ref, bf16[2048,12288]{1,0:T(8,128)(2,1)} %w_ref.11, ...), custom_call_target="tpu_custom_call", output_to_operand_aliasing={{1}: (4, {})} | custom-call | flops 17179869184 | bytes 50331648 | tf_op jit(solution)/shard_map/pallas_call | solution.py:358
  403.9 7.2 %shard_map.98 = (f32[256,2048]{1,0:T(8,128)}, f32[8,2048]{1,0:T(8,128)}) custom-call(bf16[1024,2048]{1,0:T(8,128)(2,1)} %bitcast.11, f32[1024,2048]{1,0:T(8,128)} %get-tuple-element.42.dx_any.own_ref, f32[4,256,2048]{2,1,0:T(8,128)} %get-tuple-element.48.got_ref, f32[1,2048]{1,0:T(1,128)} %bitcast.14), custom_call_target="tpu_custom_call" | custom-call | flops 134217728 | bytes 12582912 | tf_op jit(solution)/shard_map/pallas_call | solution.py:662
  411.1 162.6 %shard_map.99 = (f32[2048,7168]{1,0:T(8,128)}, f32[4,256,2048]{2,1,0:T(8,128)}, f32[8,2048]{1,0:T(8,128)}) custom-call(bf16[8192,2048]{1,0:T(8,128)(2,1)} %get-tuple-element.45.x_ref, f32[8,8,1024]{2,1,0:T(8,128)} %get-tuple-element.40.meta_ref, bf16[2048,12288]{1,0:T(8,128)(2,1)} %w_ref.11, f32[2048,4096]{1,0:T(8,128)} %get-tuple-element.43.init_ref.init_any, ...), custom_call_target="tpu_custom_call" | custom-call | flops 120259084288 | bytes 117440512 | tf_op jit(solution)/shard_map/pallas_call | solution.py:534
  573.7 1.4 slice.32
  575.1 93.1 %shard_map.100 = (f32[2048,12288]{1,0:T(8,128)}, bf16[1024,2048]{1,0:T(8,128)(2,1)}) custom-call(bf16[8192,2048]{1,0:T(8,128)(2,1)} %get-tuple-element.45.x_ref, f32[8,8,1024]{2,1,0:T(8,128)} %get-tuple-element.40.meta_ref, bf16[2048,12288]{1,0:T(8,128)(2,1)} %w_ref.11, f32[2048,7168]{1,0:T(8,128)} %get-tuple-element.51.f_any, ...), custom_call_target="tpu_custom_call" | custom-call | flops 68719476736 | bytes 201326592 | tf_op jit(solution)/shard_map/pallas_call | solution.py:619
  (15 shorter events, 0.1 us)
Async XLA Ops:
  7.2 171.3 %all-gather.6.cloned.1.call-start = ((), (), s32[]{:S(2)}) async-start(), calls=%async_computation.1 | async-start | bytes 37748736 | tf_op jit(solution)/shard_map/all_gather | solution.py:692
  12.3 5.3 copy-start
  12.3 7.6 %copy-start.1 = (s32[32]{0:T(128)S(1)}, s32[32]{0:T(128)}, u32[]{:S(2)}) copy-start(s32[32]{0:T(128)} %param.7) | copy-start | bytes 388
  12.3 364.1 %all-gather.4.cloned.1.call-start = ((), (), s32[]{:S(2)}) async-start(), calls=%async_computation | async-start | bytes 37748736 | tf_op jit(solution)/shard_map/all_gather | solution.py:694
  17.5 557.6 %all-gather.8.cloned.1.call-start = ((), (), s32[]{:S(2)}) async-start(), calls=%async_computation.2 | async-start | bytes 37748736 | tf_op jit(solution)/shard_map/all_gather | solution.py:714
  17.8 3.8 collective-permute-start
Sparse Core Ops, SparseCore 0:
  12.5 165.9 all-gather.5
  180.3 160.6 all-gather.3
  404.0 163.8 all-gather.7

commit v2 on v1

--- a/solution.py
+++ b/solution.py
@@ -242,7 +242,7 @@
     n_tok = rows // TOK
     sub = d_x_norm.shape[0] // n_tp
 
-    def kernel(x_ref, meta_ref, w_ref, dx_any, acc_ref, xb_ref, got_any, leg, mid, send_sem, recv_sem, leg_sem, mid_sem):
+    def kernel(x_ref, meta_ref, w_ref, dx_any, acc_ref, got_any, leg, mid, send_sem, recv_sem, leg_sem, mid_sem):
         b, i = pl.program_id(0), pl.program_id(1)
         step = b * n_tok + i
         stage = [split.n * n_tok * part // 32 for part in (10, 12)]
@@ -297,14 +297,8 @@
         def _():
             acc_ref[...] = jnp.zeros_like(acc_ref)
 
-        x_b = x_ref[...].astype(BF16)
-
-        @pl.when(b == 0)
-        def _():
-            xb_ref[...] = x_b
-
         first = tp * split.vocab + split.block(b, me, lax.axis_index('dp') % 2) * COLS
-        acc_ref[...] += _part(x_b, meta_ref, w_ref[...], first)
+        acc_ref[...] += _part(x_ref[...].astype(BF16), meta_ref, w_ref[...], first)
 
         @pl.when((b == split.n - 1) & (i == n_tok - 1))
         def _():
@@ -326,56 +320,55 @@
     return pl.pallas_call(
         kernel,
         grid=(split.n, n_tok),
-        out_shape=[jax.ShapeDtypeStruct((width, split.n * COLS), F32), jax.ShapeDtypeStruct((2 * rows, width), BF16), jax.ShapeDtypeStruct((n_tp, sub, width), F32)],
+        out_shape=[jax.ShapeDtypeStruct((width, split.n * COLS), F32), jax.ShapeDtypeStruct((n_tp, sub, width), F32)],
         in_specs=[
             pl.BlockSpec((TOK, width), lambda b, i: (i, 0)),
             pl.BlockSpec((TOK // half, 8, half), lambda b, i: (i, 0, 0)),
             pl.BlockSpec((width, COLS), lambda b, i: (0, split.block(b, _plane(n_dp)[0], lax.axis_index('dp') % 2))),
             _any(),
         ],
-        out_specs=[pl.BlockSpec((width, COLS), lambda b, i: (0, b)), pl.BlockSpec((TOK, width), lambda b, i: (jnp.where(b == 0, i, n_tok - 1), 0)), _any()],
+        out_specs=[pl.BlockSpec((width, COLS), lambda b, i: (0, b)), _any()],
         scratch_shapes=[pltpu.VMEM((sub, width), F32)] * 2 + [pltpu.SemaphoreType.DMA((n_tp,))] * 2 + [pltpu.SemaphoreType.DMA((2,)), pltpu.SemaphoreType.DMA],
         compiler_params=_params(collective_id=3, has_side_effects=True),
         cost_estimate=_cost(4 * rows * width * split.n * COLS, split.n * rows * width * 4),
     )(x, meta, w, d_x_norm)
 
 
-def _head_g(x, meta, w, part, x_all, split, n_dp):
+def _head_g(x_first, x, meta, w, part, split, n_dp):
     rows, width = x.shape
     half = meta.shape[2] // 2
-    n_tok = rows // half
-
-    def kernel(x_ref, meta_ref, w_ref, init_ref, _, acc_ref, xb_ref):
+
+    def kernel(xa_ref, x_ref, meta_ref, w_ref, init_ref, acc_ref, xb_ref):
         @pl.when(pl.program_id(0) == 0)
         def _():
             acc_ref[...] = init_ref[...]
 
         x_b = x_ref[...].astype(BF16)
-        xb_ref[...] = x_b
+        xb_ref[0] = xa_ref[...].astype(BF16)
+        xb_ref[1] = x_b
         first = lax.axis_index('tp') * split.vocab + (split.g0 + _plane(n_dp)[0]) * COLS
         acc_ref[...] += _part(x_b, meta_ref, w_ref[...], first)
 
+    tile = pl.BlockSpec((half, width), lambda i: (i, 0))
     return pl.pallas_call(
         kernel,
-        grid=(n_tok,),
-        out_shape=[jax.ShapeDtypeStruct((width, COLS), F32), jax.ShapeDtypeStruct((2 * rows, width), BF16)],
+        grid=(rows // half,),
+        out_shape=[jax.ShapeDtypeStruct((width, COLS), F32), jax.ShapeDtypeStruct((2, rows, width), BF16)],
         in_specs=[
-            pl.BlockSpec((half, width), lambda i: (i, 0)),
+            tile,
+            tile,
             pl.BlockSpec((1, 8, half), lambda i: (i, 0, 1)),
             pl.BlockSpec((width, COLS), lambda i: (0, split.g0 + _plane(n_dp)[0])),
             _whole((width, COLS)),
-            _any(),
         ],
-        out_specs=[_whole((width, COLS)), pl.BlockSpec((half, width), lambda i: (n_tok + i, 0))],
-        input_output_aliases={4: 1},
+        out_specs=[_whole((width, COLS)), pl.BlockSpec((2, half, width), lambda i: (0, i, 0))],
         compiler_params=_params(),
         cost_estimate=_cost(4 * rows * width * COLS, rows * width * 6),
-    )(x, meta, w, part, x_all)
+    )(x_first, x, meta, w, part)
 
 
 def _head_f(x, meta, w, part, d_hid, d_gain, split, n_tp, n_cp, n_dp):
-    width = x.shape[1]
-    rows = x.shape[0] // 2
+    _, rows, width = x.shape
     half = meta.shape[2] // 2
     n_f, groups = split.n_f, n_cp * n_dp
     n_tok = rows // TOK
@@ -493,7 +486,7 @@
                 init(j + 1).start()
 
         first = tp * split.vocab + (core * n_f + j) * COLS
-        acc[slot] += _part(x_ref[...], meta_ref, w_ref[...], first)
+        acc[slot] += _part(x_ref[0], meta_ref, w_ref[...], first)
 
         @pl.when(i == n_tok - 1)
         def _():
@@ -536,7 +529,7 @@
         grid=(n_f, n_tok),
         out_shape=[jax.ShapeDtypeStruct((width, 2 * n_f * COLS), F32), jax.ShapeDtypeStruct((n_tp, sub, width), F32), jax.ShapeDtypeStruct((8, width), F32)],
         in_specs=[
-            pl.BlockSpec((TOK, width), lambda j, i: (n_tok + i, 0)),
+            pl.BlockSpec((1, TOK, width), lambda j, i: (1, i, 0)),
             pl.BlockSpec((TOK // half, 8, half), lambda j, i: (i, 0, 1)),
             pl.BlockSpec((width, COLS), lambda j, i: (0, lax.axis_index('dp') % 2 * n_f + j)),
             _any(),
@@ -553,7 +546,7 @@
 
 
 def _head_r(x, meta, w, head_f, head_g, d_hid, d_hid_all, split, n_tp):
-    rows, width = x.shape
+    _, rows, width = x.shape
     half = meta.shape[2] // 2
     vocab, groups = split.vocab, split.groups
     steps = 2 * groups
@@ -605,7 +598,7 @@
             each(load(i), 'start')
 
         hid_ref[...] = jnp.where(i // per_q == lax.axis_index('tp'), dh_ref[...], dhall_ref[0]).astype(BF16)
-        acc[...] += _part(x_ref[...], meta_ref, w_ref[...], lax.axis_index('tp') * vocab + split.r0 * COLS)
+        acc[...] += _part(x_ref[0], meta_ref, w_ref[...], lax.axis_index('tp') * vocab + split.r0 * COLS)
 
         @pl.when(i == steps - 1)
         def _():
@@ -621,7 +614,7 @@
         grid=(steps,),
         out_shape=[jax.ShapeDtypeStruct((width, vocab), F32), jax.ShapeDtypeStruct((n_tp * sub, width), BF16)],
         in_specs=[
-            pl.BlockSpec((half, width), lambda i: (i, 0)),
+            pl.BlockSpec((1, half, width), lambda i: (i // groups, i % groups, 0)),
             pl.BlockSpec((1, 8, half), lambda i: (i % groups, 0, i // groups)),
             pl.BlockSpec((width, r_wide), lambda i: (0, split.r0 // 2)),
             _any(),
@@ -633,7 +626,7 @@
         scratch_shapes=[pltpu.VMEM((width, r_wide), F32), pltpu.VMEM((2, strip, f_wide), F32), pltpu.VMEM((2, width // 2, COLS), F32)]
         + [pltpu.SemaphoreType.DMA] + [pltpu.SemaphoreType.DMA((2, 2))] * 2,
         compiler_params=_params(),
-        cost_estimate=_cost(4 * rows * width * r_wide, width * vocab * 8),
+        cost_estimate=_cost(8 * rows * width * r_wide, width * vocab * 8),
     )(x, meta, w, head_f, head_g, d_hid, d_hid_all)
 
 
@@ -708,8 +701,8 @@
         tok_loss = meta_row[3].reshape(n_seq, local_len)
         loss_mean = jnp.sum(meta[:, 3]) / meta[0, 4, 0]
         meta, tok_loss, loss_mean = lax.optimization_barrier((meta, tok_loss, loss_mean))
-        part, x_all, got = _head_a(x_a, meta, w_head, d_x_norm, split, n_tp, n_dp)
-        d_head_g, x_all = _head_g(x_b, meta, w_head, part, x_all, split, n_dp)
+        part, got = _head_a(x_a, meta, w_head, d_x_norm, split, n_tp, n_dp)
+        d_head_g, x_all = _head_g(x_a, x_b, meta, w_head, part, split, n_dp)
         got, d_head_g = lax.optimization_barrier((got, d_head_g))
         d_head_g = lax.all_gather(d_head_g, ('cp', 'dp'), axis=0, tiled=True)
         d_hid, d_gain = _finish(hidden_rows, d_x_norm, got, gain, n_tp)

time: 677 us -> 667 us (0.985)
  Pallas kernels: 648 us -> 638 us
    pallas_call x1, Pallas kernels: 198 us -> 170 us  [_head_a(): pl.pallas_call(kernel, grid=(split.n, n_tok), out_shape=[jax.ShapeDtypeSt...]
    pallas_call x1, Pallas kernels: 27.4 us -> 44.9 us  [_head_g(): pl.pallas_call(kernel, grid=(rows // half,), out_shape=[jax.ShapeDtypeStr...]
  transfers between devices with their start and end apart: 4 -> 4, of which waited for: 0 -> 1; matrix products, arithmetic and copies ran while one was open for 1% -> 1% of each run, Pallas kernels for 77% -> 74%
where the time goes in v2:
time: 667 us; the launch traced here: 666 us
  Pallas kernels  638 us (96%)
  between operations  17 us (3%)
    pallas_call x1, Pallas kernels, _head_a(): pl.pallas_call(kernel, grid=(split.n, n_tok), out_shape=[jax.ShapeDtypeSt...  170 us
    pallas_call x1, Pallas kernels, _head_f(): pl.pallas_call(kernel, grid=(n_f, n_tok), out_shape=[jax.ShapeDtypeStruct...  162 us
    pallas_call x1, Pallas kernels, _head_r(): pl.pallas_call(kernel, grid=(steps,), out_shape=[jax.ShapeDtypeStruct((wi...  93.1 us
    pallas_call x1, Pallas kernels, _logits(): pl.pallas_call(kernel, grid=(steps,), out_shape=[jax.ShapeDtypeStruct((ro...  77.3 us
    pallas_call x1, Pallas kernels, _d_norm(): pl.pallas_call(kernel, grid=(steps,), out_shape=[jax.ShapeDtypeStruct((ro...  72.3 us
    pallas_call x1, Pallas kernels, _head_g(): pl.pallas_call(kernel, grid=(rows // half,), out_shape=[jax.ShapeDtypeStr...  44.9 us
  transfers between devices with their start and end apart: 4, of which 1 were waited for; matrix products, arithmetic and copies ran while one was open for 1% of the time, Pallas kernels for 74%

profile of v2, /device:TPU:1, one launch (start us, length us, event | category | flops | bytes accessed | tf_op | source)
XLA Modules:
  0.0 665.8 jit_solution(12418054047572560493)
XLA Ops:
  7.2 0.0 all-gather.4.cloned.1.call-start
  7.2 5.1 shard_map.92
  12.3 0.0 all-gather.6.cloned.1.call-start
  12.4 5.1 shard_map.93
  17.5 0.0 all-gather.8.cloned.1.call-start
  17.6 0.2 slice_reduce_fusion.1
  17.8 2.1 collective-permute-start
  19.9 0.6 add_reduce_fusion
  21.2 0.1 add_add_fusion
  21.3 0.1 compare_convert_fusion
  21.4 0.1 reshape.77
  21.5 0.1 fusion.2
  21.6 0.1 pad.2.clone
  21.6 0.1 copy.13
  21.7 0.1 copy.14
  21.8 0.1 add_convert_fusion
  21.9 0.1 convert_element_type.30
  22.0 0.7 maximum_maximum_fusion.row_ref
  22.7 0.6 broadcast_in_dim.22.cnt_ref.cnt_any
  23.3 77.3 %shard_map.94 = (f32[1024,12288]{1,0:T(8,128)}, f32[8,1024]{1,0:T(8,128)}, f32[1024,128]{1,0:T(8,128)}) custom-call(bf16[1024,2048]{1,0:T(8,128)(2,1)} %get-tuple-element.31.x_ref, f32[8,1024]{1,0:T(8,128)} %maximum_maximum_fusion.row_ref, f32[8,128]{1,0:T(8,128)} %broadcast_in_dim.22.cnt_ref.cnt_any, f32[8,128]{1,0:T(8,128)} %broadcast_in_dim.22.cnt_ref.cnt_any, ...), custom_call_target="tpu_custom_call" | custom-call | flops 51539607552 | bytes 100663296 | tf_op jit(solution)/shard_map/pallas_call | solution.py:154
  100.5 72.3 %shard_map.95 = (f32[1024,2048]{1,0:T(8,128)}, f32[8,8,1024]{2,1,0:T(8,128)}) custom-call(f32[1024,12288]{1,0:T(8,128)} %get-tuple-element.32.z_ref, f32[1024,128]{1,0:T(8,128)} %get-tuple-element.33.mcol_ref, f32[8,1024]{1,0:T(8,128)} %get-tuple-element.34.mrow_any, bf16[2048,12288]{1,0:T(8,128)(2,1)} %w_ref.11), custom_call_target="tpu_custom_call" | custom-call | flops 51539607552 | bytes 100663296 | tf_op jit(solution)/shard_map/pallas_call | solution.py:208
  172.8 1.2 slice.31
  174.0 0.8 slice_reduce_fusion.3
  174.8 0.7 reshape_squeeze.3
  175.5 1.6 slice_reduce_fusion
  178.4 0.1 all-gather.4.cloned.1.call-done.x_ref.xa_ref
  178.5 170.1 %shard_map.96 = (f32[2048,4096]{1,0:T(8,128)}, f32[4,256,2048]{2,1,0:T(8,128)}) custom-call(f32[4096,2048]{1,0:T(8,128)} %all-gather.4.cloned.1.call-done.x_ref.xa_ref, f32[8,8,1024]{2,1,0:T(8,128)} %get-tuple-element.40.meta_ref, bf16[2048,12288]{1,0:T(8,128)(2,1)} %w_ref.11, f32[1024,2048]{1,0:T(8,128)} %get-tuple-element.41.dx_any.own_ref), custom_call_target="tpu_custom_call" | custom-call | flops 137438953472 | bytes 268435456 | tf_op jit(solution)/shard_map/pallas_call | solution.py:320
  348.6 44.9 %shard_map.97 = (f32[2048,512]{1,0:T(8,128)}, bf16[2,4096,2048]{2,1,0:T(8,128)(2,1)}) custom-call(f32[4096,2048]{1,0:T(8,128)} %all-gather.4.cloned.1.call-done.x_ref.xa_ref, f32[4096,2048]{1,0:T(8,128)} %all-gather.6.cloned.1.call-done.x_ref, f32[8,8,1024]{2,1,0:T(8,128)} %get-tuple-element.40.meta_ref, bf16[2048,12288]{1,0:T(8,128)(2,1)} %w_ref.11, ...), custom_call_target="tpu_custom_call" | custom-call | flops 17179869184 | bytes 50331648 | tf_op jit(solution)/shard_map/pallas_call | solution.py:353
  393.5 7.6 %shard_map.98 = (f32[256,2048]{1,0:T(8,128)}, f32[8,2048]{1,0:T(8,128)}) custom-call(bf16[1024,2048]{1,0:T(8,128)(2,1)} %bitcast.11, f32[1024,2048]{1,0:T(8,128)} %get-tuple-element.41.dx_any.own_ref, f32[4,256,2048]{2,1,0:T(8,128)} %get-tuple-element.46.got_ref, f32[1,2048]{1,0:T(1,128)} %bitcast.14), custom_call_target="tpu_custom_call" | custom-call | flops 134217728 | bytes 12582912 | tf_op jit(solution)/shard_map/pallas_call | solution.py:655
  401.2 162.5 %shard_map.99 = (f32[2048,7168]{1,0:T(8,128)}, f32[4,256,2048]{2,1,0:T(8,128)}, f32[8,2048]{1,0:T(8,128)}) custom-call(bf16[2,4096,2048]{2,1,0:T(8,128)(2,1)} %get-tuple-element.43.x_ref, f32[8,8,1024]{2,1,0:T(8,128)} %get-tuple-element.40.meta_ref, bf16[2048,12288]{1,0:T(8,128)(2,1)} %w_ref.11, f32[2048,4096]{1,0:T(8,128)} %get-tuple-element.42.init_ref.init_any, ...), custom_call_target="tpu_custom_call" | custom-call | flops 120259084288 | bytes 117440512 | tf_op jit(solution)/shard_map/pallas_call | solution.py:527
  563.6 1.4 slice.32
  565.1 93.1 %shard_map.100 = (f32[2048,12288]{1,0:T(8,128)}, bf16[1024,2048]{1,0:T(8,128)(2,1)}) custom-call(bf16[2,4096,2048]{2,1,0:T(8,128)(2,1)} %get-tuple-element.43.x_ref, f32[8,8,1024]{2,1,0:T(8,128)} %get-tuple-element.40.meta_ref, bf16[2048,12288]{1,0:T(8,128)(2,1)} %w_ref.11, f32[2048,7168]{1,0:T(8,128)} %get-tuple-element.49.f_any, ...), custom_call_target="tpu_custom_call" | custom-call | flops 68719476736 | bytes 201326592 | tf_op jit(solution)/shard_map/pallas_call | solution.py:612
  (15 shorter events, 0.1 us)
Async XLA Ops:
  7.2 171.3 %all-gather.4.cloned.1.call-start = ((), (), s32[]{:S(2)}) async-start(), calls=%async_computation | async-start | bytes 37748736 | tf_op jit(solution)/shard_map/all_gather | solution.py:685
  12.3 5.3 copy-start
  12.3 7.6 %copy-start.1 = (s32[32]{0:T(128)S(1)}, s32[32]{0:T(128)}, u32[]{:S(2)}) copy-start(s32[32]{0:T(128)} %param.7) | copy-start | bytes 388
  12.3 336.3 %all-gather.6.cloned.1.call-start = ((), (), s32[]{:S(2)}) async-start(), calls=%async_computation.1 | async-start | bytes 37748736 | tf_op jit(solution)/shard_map/all_gather | solution.py:687
  17.5 547.5 %all-gather.8.cloned.1.call-start = ((), (), s32[]{:S(2)}) async-start(), calls=%async_computation.2 | async-start | bytes 37748736 | tf_op jit(solution)/shard_map/all_gather | solution.py:707
  17.8 3.8 collective-permute-start
Sparse Core Ops, SparseCore 0:
  12.5 166.0 all-gather.3
  180.4 160.6 all-gather.5
  393.7 162.9 all-gather.7

commit v3 on v2

--- a/solution.py
+++ b/solution.py
@@ -334,47 +334,48 @@
     )(x, meta, w, d_x_norm)
 
 
-def _head_g(x_first, x, meta, w, part, split, n_dp):
+def _head_g(x, meta, w, part, split, n_dp):
     rows, width = x.shape
     half = meta.shape[2] // 2
 
-    def kernel(xa_ref, x_ref, meta_ref, w_ref, init_ref, acc_ref, xb_ref):
+    def kernel(x_ref, meta_ref, w_ref, init_ref, acc_ref, xb_ref):
         @pl.when(pl.program_id(0) == 0)
         def _():
             acc_ref[...] = init_ref[...]
 
         x_b = x_ref[...].astype(BF16)
-        xb_ref[0] = xa_ref[...].astype(BF16)
-        xb_ref[1] = x_b
+        xb_ref[0] = x_b
         first = lax.axis_index('tp') * split.vocab + (split.g0 + _plane(n_dp)[0]) * COLS
         acc_ref[...] += _part(x_b, meta_ref, w_ref[...], first)
 
-    tile = pl.BlockSpec((half, width), lambda i: (i, 0))
     return pl.pallas_call(
         kernel,
         grid=(rows // half,),
         out_shape=[jax.ShapeDtypeStruct((width, COLS), F32), jax.ShapeDtypeStruct((2, rows, width), BF16)],
         in_specs=[
-            tile,
-            tile,
+            pl.BlockSpec((half, width), lambda i: (i, 0)),
             pl.BlockSpec((1, 8, half), lambda i: (i, 0, 1)),
             pl.BlockSpec((width, COLS), lambda i: (0, split.g0 + _plane(n_dp)[0])),
             _whole((width, COLS)),
         ],
-        out_specs=[_whole((width, COLS)), pl.BlockSpec((2, half, width), lambda i: (0, i, 0))],
+        out_specs=[_whole((width, COLS)), pl.BlockSpec((1, half, width), lambda i: (1, i, 0))],
         compiler_params=_params(),
         cost_estimate=_cost(4 * rows * width * COLS, rows * width * 6),
-    )(x_first, x, meta, w, part)
-
-
-def _head_f(x, meta, w, part, d_hid, d_gain, split, n_tp, n_cp, n_dp):
+    )(x, meta, w, part)
+
+
+def _head_f(x, x_first, meta, w, part, d_hid, d_gain, split, n_tp, n_cp, n_dp):
     _, rows, width = x.shape
     half = meta.shape[2] // 2
     n_f, groups = split.n_f, n_cp * n_dp
     n_tok = rows // TOK
     sub = d_hid.shape[0]
-
-    def kernel(x_ref, meta_ref, w_ref, init_any, dh_any, dg_any, out_any, dhall_any, dg_ref, acc, dg_z, dg_s, dg_x, init_sem, own_sem, send_sem, recv_sem, hs_sem, hr_sem, fs_sem, zs_sem, zr_sem, zo_sem, xs_sem, xr_sem):
+    cut = TOK // 4
+
+    def turn(j, i):
+        return jnp.minimum(j * n_tok + i, rows // cut - 1)
+
+    def kernel(x_ref, xa_ref, meta_ref, w_ref, init_any, dh_any, dg_any, out_any, dhall_any, dg_ref, xo_ref, acc, dg_z, dg_s, dg_x, init_sem, own_sem, send_sem, recv_sem, hs_sem, hr_sem, fs_sem, zs_sem, zr_sem, zo_sem, xs_sem, xr_sem):
         j, i = pl.program_id(0), pl.program_id(1)
         step = j * n_tok + i
         stage = [n_f * n_tok * part // 28 for part in (9, 12, 18, 21)]
@@ -485,6 +486,7 @@
             def _():
                 init(j + 1).start()
 
+        xo_ref[0] = xa_ref[...].astype(BF16)
         first = tp * split.vocab + (core * n_f + j) * COLS
         acc[slot] += _part(x_ref[0], meta_ref, w_ref[...], first)
 
@@ -527,22 +529,24 @@
     return pl.pallas_call(
         kernel,
         grid=(n_f, n_tok),
-        out_shape=[jax.ShapeDtypeStruct((width, 2 * n_f * COLS), F32), jax.ShapeDtypeStruct((n_tp, sub, width), F32), jax.ShapeDtypeStruct((8, width), F32)],
+        out_shape=[jax.ShapeDtypeStruct((width, 2 * n_f * COLS), F32), jax.ShapeDtypeStruct((n_tp, sub, width), F32), jax.ShapeDtypeStruct((8, width), F32), jax.ShapeDtypeStruct(x.shape, BF16)],
         in_specs=[
             pl.BlockSpec((1, TOK, width), lambda j, i: (1, i, 0)),
+            pl.BlockSpec((cut, width), lambda j, i: (turn(j, i), 0)),
             pl.BlockSpec((TOK // half, 8, half), lambda j, i: (i, 0, 1)),
             pl.BlockSpec((width, COLS), lambda j, i: (0, lax.axis_index('dp') % 2 * n_f + j)),
             _any(),
             _any(),
             _any(),
         ],
-        out_specs=[_any(), _any(), _whole((8, width))],
+        out_specs=[_any(), _any(), _whole((8, width)), pl.BlockSpec((1, cut, width), lambda j, i: (0, turn(j, i), 0))],
+        input_output_aliases={0: 3},
         scratch_shapes=[pltpu.VMEM((2, width, COLS), F32), pltpu.VMEM((n_tp, 8, width), F32), pltpu.VMEM((8, width), F32), pltpu.VMEM((groups, 8, width), F32)]
         + [pltpu.SemaphoreType.DMA((2,))] * 3 + [pltpu.SemaphoreType.DMA((n_f,)), pltpu.SemaphoreType.DMA((n_tp, 2)), pltpu.SemaphoreType.DMA((n_tp, 2)), pltpu.SemaphoreType.DMA((2,))]
         + [pltpu.SemaphoreType.DMA((n_tp - 1,))] * 2 + [pltpu.SemaphoreType.DMA] + [pltpu.SemaphoreType.DMA((groups - 1,))] * 2,
         compiler_params=_params(collective_id=4, has_side_effects=True),
         cost_estimate=_cost(4 * rows * width * n_f * COLS, n_f * rows * width * 2),
-    )(x, meta, w, part, d_hid, d_gain)
+    )(x, x_first, meta, w, part, d_hid, d_gain)
 
 
 def _head_r(x, meta, w, head_f, head_g, d_hid, d_hid_all, split, n_tp):
@@ -702,11 +706,11 @@
         loss_mean = jnp.sum(meta[:, 3]) / meta[0, 4, 0]
         meta, tok_loss, loss_mean = lax.optimization_barrier((meta, tok_loss, loss_mean))
         part, got = _head_a(x_a, meta, w_head, d_x_norm, split, n_tp, n_dp)
-        d_head_g, x_all = _head_g(x_a, x_b, meta, w_head, part, split, n_dp)
+        d_head_g, x_all = _head_g(x_b, meta, w_head, part, split, n_dp)
         got, d_head_g = lax.optimization_barrier((got, d_head_g))
         d_head_g = lax.all_gather(d_head_g, ('cp', 'dp'), axis=0, tiled=True)
         d_hid, d_gain = _finish(hidden_rows, d_x_norm, got, gain, n_tp)
-        d_head_f, d_hid_all, d_gain = _head_f(x_all, meta, w_head, part, d_hid, d_gain, split, n_tp, n_cp, n_dp)
+        d_head_f, d_hid_all, d_gain, x_all = _head_f(x_all, x_a, meta, w_head, part, d_hid, d_gain, split, n_tp, n_cp, n_dp)
         d_head, d_hidden = _head_r(x_all, meta, w_head, d_head_f, d_head_g, d_hid, d_hid_all, split, n_tp)
 
         return tok_loss, loss_mean, d_hidden.reshape(hidden.shape), d_gain[0], d_head

time: 667 us -> 656 us (0.984)
  Pallas kernels: 638 us -> 627 us
    pallas_call x1, Pallas kernels: 44.9 us -> 27.3 us  [_head_g(): pl.pallas_call(kernel, grid=(rows // half,), out_shape=[jax.ShapeDtypeStr...]
  transfers between devices with their start and end apart: 4 -> 4, of which waited for: 1 -> 1; matrix products, arithmetic and copies ran while one was open for 1% -> 1% of each run, Pallas kernels for 74% -> 77%
where the time goes in v3:
time: 656 us; the launch traced here: 655 us
  Pallas kernels  627 us (96%)
  between operations  17 us (3%)
    pallas_call x1, Pallas kernels, _head_a(): pl.pallas_call(kernel, grid=(split.n, n_tok), out_shape=[jax.ShapeDtypeSt...  170 us
    pallas_call x1, Pallas kernels, _head_f(): pl.pallas_call(kernel, grid=(n_f, n_tok), out_shape=[jax.ShapeDtypeStruct...  169 us
    pallas_call x1, Pallas kernels, _head_r(): pl.pallas_call(kernel, grid=(steps,), out_shape=[jax.ShapeDtypeStruct((wi...  93.1 us
    pallas_call x1, Pallas kernels, _logits(): pl.pallas_call(kernel, grid=(steps,), out_shape=[jax.ShapeDtypeStruct((ro...  77.2 us
    pallas_call x1, Pallas kernels, _d_norm(): pl.pallas_call(kernel, grid=(steps,), out_shape=[jax.ShapeDtypeStruct((ro...  72.3 us
    pallas_call x1, Pallas kernels, _head_g(): pl.pallas_call(kernel, grid=(rows // half,), out_shape=[jax.ShapeDtypeStr...  27.3 us
  transfers between devices with their start and end apart: 4, of which 1 were waited for; matrix products, arithmetic and copies ran while one was open for 1% of the time, Pallas kernels for 77%

profile of v3, /device:TPU:1, one launch (start us, length us, event | category | flops | bytes accessed | tf_op | source)
XLA Modules:
  0.0 654.9 jit_solution(13510504570536613302)
XLA Ops:
  7.2 0.0 all-gather.6.cloned.1.call-start
  7.2 5.1 shard_map.92
  12.3 0.0 all-gather.4.cloned.1.call-start
  12.4 5.1 shard_map.93
  17.6 0.0 all-gather.8.cloned.1.call-start
  17.6 0.2 slice_reduce_fusion.1
  17.8 2.1 collective-permute-start
  19.9 0.6 add_reduce_fusion
  21.3 0.1 add_add_fusion
  21.3 0.1 compare_convert_fusion
  21.4 0.1 reshape.77
  21.5 0.1 fusion.2
  21.6 0.1 pad.2.clone
  21.6 0.1 copy.14
  21.7 0.1 copy.15
  21.8 0.1 add_convert_fusion
  21.9 0.1 convert_element_type.30
  22.0 0.7 maximum_maximum_fusion.row_ref
  22.7 0.6 broadcast_in_dim.22.cnt_ref.cnt_any
  23.3 77.2 %shard_map.94 = (f32[1024,12288]{1,0:T(8,128)}, f32[8,1024]{1,0:T(8,128)}, f32[1024,128]{1,0:T(8,128)}) custom-call(bf16[1024,2048]{1,0:T(8,128)(2,1)} %get-tuple-element.32.x_ref, f32[8,1024]{1,0:T(8,128)} %maximum_maximum_fusion.row_ref, f32[8,128]{1,0:T(8,128)} %broadcast_in_dim.22.cnt_ref.cnt_any, f32[8,128]{1,0:T(8,128)} %broadcast_in_dim.22.cnt_ref.cnt_any, ...), custom_call_target="tpu_custom_call" | custom-call | flops 51539607552 | bytes 100663296 | tf_op jit(solution)/shard_map/pallas_call | solution.py:154
  100.5 72.3 %shard_map.95 = (f32[1024,2048]{1,0:T(8,128)}, f32[8,8,1024]{2,1,0:T(8,128)}) custom-call(f32[1024,12288]{1,0:T(8,128)} %get-tuple-element.33.z_ref, f32[1024,128]{1,0:T(8,128)} %get-tuple-element.34.mcol_ref, f32[8,1024]{1,0:T(8,128)} %get-tuple-element.35.mrow_any, bf16[2048,12288]{1,0:T(8,128)(2,1)} %w_ref.11), custom_call_target="tpu_custom_call" | custom-call | flops 51539607552 | bytes 100663296 | tf_op jit(solution)/shard_map/pallas_call | solution.py:208
  172.8 1.2 slice.31
  174.0 0.8 slice_reduce_fusion.3
  174.8 0.7 reshape_squeeze.3
  175.5 1.6 slice_reduce_fusion
  178.4 0.1 all-gather.6.cloned.1.call-done.x_ref.xa_ref
  178.5 170.1 %shard_map.96 = (f32[2048,4096]{1,0:T(8,128)}, f32[4,256,2048]{2,1,0:T(8,128)}) custom-call(f32[4096,2048]{1,0:T(8,128)} %all-gather.6.cloned.1.call-done.x_ref.xa_ref, f32[8,8,1024]{2,1,0:T(8,128)} %get-tuple-element.40.meta_ref, bf16[2048,12288]{1,0:T(8,128)(2,1)} %w_ref.11, f32[1024,2048]{1,0:T(8,128)} %get-tuple-element.42.dx_any.own_ref), custom_call_target="tpu_custom_call" | custom-call | flops 137438953472 | bytes 268435456 | tf_op jit(solution)/shard_map/pallas_call | solution.py:320
  348.6 27.3 %shard_map.97 = (f32[2048,512]{1,0:T(8,128)}, bf16[2,4096,2048]{2,1,0:T(8,128)(2,1)}) custom-call(f32[4096,2048]{1,0:T(8,128)} %all-gather.4.cloned.1.call-done.x_ref, f32[8,8,1024]{2,1,0:T(8,128)} %get-tuple-element.40.meta_ref, bf16[2048,12288]{1,0:T(8,128)(2,1)} %w_ref.11, f32[2048,4096]{1,0:T(8,128)} %get-tuple-element.43.init_ref.init_any), custom_call_target="tpu_custom_call" | custom-call | flops 17179869184 | bytes 50331648 | tf_op jit(solution)/shard_map/pallas_call | solution.py:351
  376.0 7.6 %shard_map.98 = (f32[256,2048]{1,0:T(8,128)}, f32[8,2048]{1,0:T(8,128)}) custom-call(bf16[1024,2048]{1,0:T(8,128)(2,1)} %bitcast.11, f32[1024,2048]{1,0:T(8,128)} %get-tuple-element.42.dx_any.own_ref, f32[4,256,2048]{2,1,0:T(8,128)} %get-tuple-element.47.got_ref, f32[1,2048]{1,0:T(1,128)} %bitcast.14), custom_call_target="tpu_custom_call" | custom-call | flops 134217728 | bytes 12582912 | tf_op jit(solution)/shard_map/pallas_call | solution.py:659
  383.6 169.1 %shard_map.99 = (f32[2048,7168]{1,0:T(8,128)}, f32[4,256,2048]{2,1,0:T(8,128)}, f32[8,2048]{1,0:T(8,128)}, bf16[2,4096,2048]{2,1,0:T(8,128)(2,1)}) custom-call(bf16[2,4096,2048]{2,1,0:T(8,128)(2,1)} %get-tuple-element.44.x_ref, f32[4096,2048]{1,0:T(8,128)} %all-gather.6.cloned.1.call-done.x_ref.xa_ref, ...), custom_call_target="tpu_custom_call", output_to_operand_aliasing={{3}: (0, {})} | custom-call | flops 120259084288 | bytes 117440512 | tf_op jit(solution)/shard_map/pallas_call | solution.py:529
  552.7 1.4 slice.32
  554.2 93.1 %shard_map.100 = (f32[2048,12288]{1,0:T(8,128)}, bf16[1024,2048]{1,0:T(8,128)(2,1)}) custom-call(bf16[2,4096,2048]{2,1,0:T(8,128)(2,1)} %get-tuple-element.50.x_ref, f32[8,8,1024]{2,1,0:T(8,128)} %get-tuple-element.40.meta_ref, bf16[2048,12288]{1,0:T(8,128)(2,1)} %w_ref.11, f32[2048,7168]{1,0:T(8,128)} %get-tuple-element.51.f_any, ...), custom_call_target="tpu_custom_call" | custom-call | flops 68719476736 | bytes 201326592 | tf_op jit(solution)/shard_map/pallas_call | solution.py:616
  (15 shorter events, 0.1 us)
Async XLA Ops:
  7.2 171.3 %all-gather.6.cloned.1.call-start = ((), (), s32[]{:S(2)}) async-start(), calls=%async_computation.1 | async-start | bytes 37748736 | tf_op jit(solution)/shard_map/all_gather | solution.py:689
  12.3 5.3 copy-start
  12.3 7.6 %copy-start.1 = (s32[32]{0:T(128)S(1)}, s32[32]{0:T(128)}, u32[]{:S(2)}) copy-start(s32[32]{0:T(128)} %param.7) | copy-start | bytes 388
  12.3 336.3 %all-gather.4.cloned.1.call-start = ((), (), s32[]{:S(2)}) async-start(), calls=%async_computation | async-start | bytes 37748736 | tf_op jit(solution)/shard_map/all_gather | solution.py:691
  17.6 536.6 %all-gather.8.cloned.1.call-start = ((), (), s32[]{:S(2)}) async-start(), calls=%async_computation.2 | async-start | bytes 37748736 | tf_op jit(solution)/shard_map/all_gather | solution.py:711
  17.8 3.8 collective-permute-start
Sparse Core Ops, SparseCore 0:
  12.5 166.0 all-gather.5
  180.4 160.6 all-gather.3
  376.1 161.6 all-gather.7
